TPU v7x, 32 devices: a whole 2x2x4 slice. The times are simulated.
32 devices in a mesh: dp: 8 (over z, x), rep: 4 (over y, core).
Axes of the slice: x: 2, y: 2, z: 4, core: 2. Of those that a mesh axis runs over, the one named last changes fastest.
Arguments:
- features: bfloat16 [5120, 8192], P('dp', 'rep'), may hold values from -6 to 6
- out_grads: bfloat16 [5120, 1024], P('dp'), may hold values from -12 to 12, as said below
- cold_sums: bfloat16 [8, 8192, 1024], P('dp', 'rep'), may hold values from -96 to 96
- weight: float32 [8192, 1024], P(('rep', 'dp')), may hold values from -3 to 3
- moment: float32 [8192, 1024], P(('rep', 'dp')), may hold values from -6 to 6
- second: float32 [8192, 1024], P(('rep', 'dp')), may hold values from 0.01 to 4
- ranks: int32 [8], replicated, may hold values from 0 to 7, each once
Outputs:
- new_weight: float32 [8192, 1024], P(('rep', 'dp'))
- new_moment: float32 [8192, 1024], P(('rep', 'dp'))
- new_second: float32 [8192, 1024], P(('rep', 'dp'))
- new_cold: bfloat16 [8, 8192, 1024], P('dp', 'rep')
- column_sq: float32 [1024], replicated
Inputs may be any that keep to these rules, and one draw needn't show every extreme that they name: `ranks`: each block number appears once. `out_grads`: column scales differ from column to column.
All inputs are finite; a program needn't handle non-finite values.
Results may differ from a plain program's by a relative error of at most 0.001.
Values sent between devices are 32-bit elements; how exact they have to be, the bound alone decides.
A program may use at most 128 MiB of HBM per device.

v0:
```python
import functools
import jax
import jax.numpy as jnp
from jax import lax
from jax.experimental import pallas as pl
from jax.experimental.pallas import tpu as pltpu
from jax.sharding import PartitionSpec as P

LANES = 128
SUB = 2
VMEM_GRANT = 30 * 2**20
MESH = pl.DeviceIdType.MESH


def bits_of(size):
    return max(size.bit_length() - 1, 0)


def flipped(index, bit):
    step = 1 << bit
    return index + step - 2 * step * ((index // step) % 2)


def exchange_kernel(
    n, reps, hot,
    ranks, feat, og, cold, weight, moment, second,
    summed, sq_out, nc_out, w_out, m_out, s_out,
    feat_v, og_v, cold_v, local, pack, rx, lbuf, rbuf, hsrc, hbuf,
    in_sem, state_sem, send1, recv1, zsend, lrecv, rrecv, hsend, hrecv,
):
    m = n // 2
    rows, width = cold.shape[1], cold.shape[2]
    blocks = width // LANES
    own = rows // n
    chunk = max(own, LANES)
    chunks = rows // chunk
    part = own // SUB
    me = lax.axis_index("dp")
    rep = lax.axis_index("rep")
    x = me % 2
    p = me // 2
    partner = me + 1 - 2 * x
    dp_bits, rep_bits = bits_of(n), bits_of(reps)
    steps = [("dp", b) for b in range(dp_bits)] + [("rep", b) for b in range(rep_bits)]

    half = max(m // 2, 1)
    flip = p // half if m > 1 else 0
    pr = p + flip * (m - 1 - 2 * p)

    def dest(k):
        if m == 1:
            return 0 * k
        late = (k + pr) // (m - 1)
        near = (1 - late) * (m - 1 - k) + late * (k + pr - (m - 1))
        last = k // (m - 1)
        near = (1 - last) * near + last * pr
        return near + flip * (m - 1 - 2 * near)

    def chunk_at(i):
        if chunk != own:
            return i
        k = i % m
        side = i // m
        return 2 * dest(k) + (1 - side) * (1 - x) + side * x

    def hop(axis, b):
        index = me if axis == "dp" else rep
        return {axis: flipped(index, b)}

    barrier = pltpu.get_barrier_semaphore()
    pl.semaphore_signal(barrier, inc=1, device_id={"dp": partner}, device_id_type=MESH)

    @pl.when(p > 0)
    def _():
        pl.semaphore_signal(barrier, inc=1, device_id={"dp": me - 2}, device_id_type=MESH)

    @pl.when(p < m - 1)
    def _():
        pl.semaphore_signal(barrier, inc=1, device_id={"dp": me + 2}, device_id_type=MESH)

    for axis, b in steps[1:]:
        pl.semaphore_signal(barrier, inc=1, device_id=hop(axis, b), device_id_type=MESH)

    def feat_copy(i):
        c = chunk_at(i)
        cols = pl.ds(pl.multiple_of(c * chunk, LANES), chunk)
        return pltpu.make_async_copy(feat.at[:, cols], feat_v.at[i], in_sem.at[0, i])

    def cold_copy(i):
        c = chunk_at(i)
        at = pl.ds(pl.multiple_of(c * chunk, LANES), chunk)
        return pltpu.make_async_copy(cold.at[0, at], cold_v.at[i], in_sem.at[1, i])

    state = [
        pltpu.make_async_copy(src, dst, state_sem.at[i])
        for i, (src, dst) in enumerate(
            ((weight, w_out), (moment, m_out), (second, s_out), (og, og_v))
        )
    ]
    feat_copy(0).start()
    state[3].start()
    cold_copy(0).start()

    def fetch(i, carry):
        feat_copy(i).start()
        cold_copy(i).start()
        return carry

    lax.fori_loop(1, chunks, fetch, 0)
    for copy in state[:3]:
        copy.start()

    hsrc[0] = jnp.zeros_like(hsrc[0])
    keep = [
        jnp.minimum(jnp.maximum(ranks[b] - (hot - 1), 0), 1).astype(jnp.float32)
        for b in range(blocks)
    ]
    picks = []
    for s in range(hot):
        row = []
        for b in range(blocks):
            gap = ranks[b] - s
            row.append((1 - jnp.minimum(gap * gap, 1)).astype(jnp.float32))
        picks.append(row)

    def cross(k, sub):
        d = dest(k)
        src = pl.ds(pl.multiple_of((2 * d + 1 - x) * own + sub * part, 8), part)
        dst = pl.ds(pl.multiple_of(d * own + sub * part, 8), part)
        return pltpu.make_async_remote_copy(
            src_ref=pack.at[src], dst_ref=rx.at[dst],
            send_sem=send1.at[d, sub], recv_sem=recv1.at[d, sub],
            device_id={"dp": partner}, device_id_type=MESH,
        )

    def along(d, sub, right):
        src = pl.ds(pl.multiple_of((2 * d + x) * own + sub * part, 8), part)
        dst = pl.ds(pl.multiple_of(d * own + sub * part, 8), part)
        return pltpu.make_async_remote_copy(
            src_ref=pack.at[src], dst_ref=(lbuf if right else rbuf).at[dst],
            send_sem=zsend.at[d, sub], recv_sem=(lrecv if right else rrecv).at[d, sub],
            device_id={"dp": me + 2 if right else me - 2}, device_id_type=MESH,
        )

    def norm_copy(s):
        return pltpu.make_async_remote_copy(
            src_ref=hsrc.at[s], dst_ref=hbuf.at[s],
            send_sem=hsend.at[s], recv_sem=hrecv.at[s],
            device_id=hop(*steps[s]), device_id_type=MESH,
        )

    greeted = 1 + (len(steps) - 1) + (p + m - 1) // m + (2 * m - 2 - p) // m
    pl.semaphore_wait(barrier, greeted)
    state[3].wait()

    def compute(i, carry):
        c = chunk_at(i)
        feat_copy(i).wait()
        cold_copy(i).wait()
        local[...] = lax.dot_general(
            feat_v[i], og_v[...], (((0,), (0,)), ((), ())),
            preferred_element_type=jnp.float32,
        ) + cold_v[i].astype(jnp.float32)
        at = pl.ds(pl.multiple_of(c * chunk, LANES), chunk)
        for s in range(hot):
            picked = local[:, :LANES] * picks[s][0]
            for b in range(1, blocks):
                picked += local[:, b * LANES:(b + 1) * LANES] * picks[s][b]
            pack[at, s * LANES:(s + 1) * LANES] = picked
        if chunk == own:
            @pl.when(i < m)
            def _():
                for sub in range(SUB):
                    cross(i % m, sub).start()
        for b in range(blocks):
            cols = slice(b * LANES, (b + 1) * LANES)
            values = local[:, cols]
            hsrc[0, b:b + 1, :] += jnp.sum(values * values, axis=0, keepdims=True)
            nc_out[0, at, cols] = (values * keep[b]).astype(jnp.bfloat16)
        return carry

    lax.fori_loop(0, chunks, compute, 0)
    if chunk != own:
        def launch(k, carry):
            for sub in range(SUB):
                cross(k, sub).start()
            return carry

        lax.fori_loop(0, m, launch, 0)
    norm_copy(0).start()

    def process(k, sub):
        d = dest(k)
        mine = pl.ds(pl.multiple_of((2 * d + x) * own + sub * part, 8), part)
        slot = pl.ds(pl.multiple_of(d * own + sub * part, 8), part)
        cross(k, sub).wait_recv()
        pack[mine] += rx[slot]

        @pl.when(jnp.logical_and(d >= p, p > 0))
        def _():
            along(d, sub, True).wait_recv()
            pack[mine] += lbuf[slot]

        @pl.when(jnp.logical_and(d <= p, p < m - 1))
        def _():
            along(d, sub, False).wait_recv()
            pack[mine] += rbuf[slot]

        @pl.when(d > p)
        def _():
            along(d, sub, True).start()

        @pl.when(d < p)
        def _():
            along(d, sub, False).start()

        @pl.when(d == p)
        def _():
            summed[sub * part:(sub + 1) * part] = pack[mine]

    def norm_step(s):
        norm_copy(s).wait_recv()
        hsrc[s + 1] = hsrc[s] + hbuf[s]
        if s + 1 < len(steps):
            norm_copy(s + 1).start()

    done = 0
    if m <= 8:
        for k in range(m):
            for sub in range(SUB):
                if done < len(steps):
                    norm_step(done)
                    done += 1
                process(k, sub)
    else:
        def walk(k, carry):
            for sub in range(SUB):
                process(k, sub)
            return carry

        lax.fori_loop(0, m, walk, 0)
    for s in range(done, len(steps)):
        norm_step(s)
    sq_out[...] = hsrc[len(steps)]

    for copy in state[:3]:
        copy.wait()

    def drain(k, carry):
        d = dest(k)
        for sub in range(SUB):
            cross(k, sub).wait_send()

            @pl.when(d > p)
            def _():
                along(d, sub, True).wait_send()

            @pl.when(d < p)
            def _():
                along(d, sub, False).wait_send()
        return carry

    lax.fori_loop(0, m, drain, 0)
    for s in range(len(steps)):
        norm_copy(s).wait_send()


def update_kernel(
    n, total_rows, tokens, hot,
    ranks, summed, sq, nc, weight, moment, second,
    w_hbm, m_hbm, s_hbm, nc_hbm,
    fresh, nc_sem, sem,
):
    rows, width = weight.shape
    blocks = width // LANES
    cold_out = pltpu.make_async_copy(nc, nc_hbm, nc_sem)
    cold_out.start()
    for b in range(blocks):
        cols = slice(b * LANES, (b + 1) * LANES)
        slot = ranks[b]

        @pl.when(slot < hot)
        def _():
            total = sq[b:b + 1, :]
            rms = jnp.sqrt(total / jnp.float32(total_rows * n * tokens))
            clip = 1.0 / jnp.maximum(jnp.float32(1.0), rms)
            at = pl.ds(pl.multiple_of(slot * LANES, LANES), LANES)
            grad = summed[:, at] * clip / jnp.float32(n)
            moved = 0.9 * moment[:, cols] + 0.1 * grad
            squared = 0.95 * second[:, cols] + 0.05 * grad * grad
            fresh[1, :, cols] = moved
            fresh[2, :, cols] = squared
            step = 0.05 * (moved / (1.0 - 0.9**10)) / (
                jnp.sqrt(squared / (1.0 - 0.95**10)) + 1e-08
            )
            fresh[0, :, cols] = weight[:, cols] - step

        @pl.when(slot >= hot)
        def _():
            fresh[0, :, cols] = weight[:, cols]
            fresh[1, :, cols] = moment[:, cols]
            fresh[2, :, cols] = second[:, cols]

    copies = [
        pltpu.make_async_copy(fresh.at[i], dst, sem.at[i])
        for i, dst in enumerate((w_hbm, m_hbm, s_hbm))
    ]
    for copy in copies:
        copy.start()
    for copy in copies:
        copy.wait()
    cold_out.wait()


def body(n, reps, features, out_grads, cold_sums, weight, moment, second, ranks):
    tokens, rows = features.shape
    width = out_grads.shape[1]
    blocks = ranks.shape[0]
    hot = blocks // 2
    packed = hot * LANES
    m = n // 2
    own = rows // n
    chunk = max(own, LANES)
    chunks = rows // chunk
    hops = bits_of(n) + bits_of(reps)
    f32, bf16 = jnp.float32, jnp.bfloat16
    vmem = pl.BlockSpec(memory_space=pltpu.VMEM)
    smem = pl.BlockSpec(memory_space=pltpu.SMEM)
    hbm = pl.BlockSpec(memory_space=pl.ANY)
    dma = pltpu.SemaphoreType.DMA
    summed, sq, kept, w, mo, se = pl.pallas_call(
        functools.partial(exchange_kernel, n, reps, hot),
        out_shape=(
            pltpu.VMEM((own, packed), f32),
            pltpu.VMEM((blocks, LANES), f32),
            pltpu.VMEM(cold_sums.shape, bf16),
            pltpu.VMEM(weight.shape, f32),
            pltpu.VMEM(weight.shape, f32),
            pltpu.VMEM(weight.shape, f32),
        ),
        in_specs=[smem] + [pl.BlockSpec(memory_space=pltpu.HBM)] * 6,
        out_specs=(vmem,) * 6,
        scratch_shapes=[
            pltpu.VMEM((chunks, tokens, chunk), bf16),
            pltpu.VMEM((tokens, width), bf16),
            pltpu.VMEM((chunks, chunk, width), bf16),
            pltpu.VMEM((chunk, width), f32),
            pltpu.VMEM((rows, packed), f32),
            pltpu.VMEM((m * own, packed), f32),
            pltpu.VMEM((m * own, packed), f32),
            pltpu.VMEM((m * own, packed), f32),
            pltpu.VMEM((hops + 1, blocks, LANES), f32),
            pltpu.VMEM((hops, blocks, LANES), f32),
            dma((2, chunks)),
            dma((4,)),
            dma((m, SUB)),
            dma((m, SUB)),
            dma((m, SUB)),
            dma((m, SUB)),
            dma((m, SUB)),
            dma((hops,)),
            dma((hops,)),
        ],
        compiler_params=pltpu.CompilerParams(
            collective_id=0, has_side_effects=True, vmem_limit_bytes=VMEM_GRANT
        ),
        name="exchange",
    )(ranks, features, out_grads, cold_sums, weight, moment, second)
    new_weight, new_moment, new_second, new_cold = pl.pallas_call(
        functools.partial(update_kernel, n, rows * reps, tokens, hot),
        out_shape=(
            jax.ShapeDtypeStruct(weight.shape, f32),
            jax.ShapeDtypeStruct(weight.shape, f32),
            jax.ShapeDtypeStruct(weight.shape, f32),
            jax.ShapeDtypeStruct(cold_sums.shape, bf16),
        ),
        in_specs=[smem] + [vmem] * 6,
        out_specs=(hbm,) * 4,
        scratch_shapes=[pltpu.VMEM((3,) + weight.shape, f32), dma, dma((3,))],
        compiler_params=pltpu.CompilerParams(vmem_limit_bytes=VMEM_GRANT),
        name="update",
    )(ranks, summed, sq, kept, w, mo, se)
    return new_weight, new_moment, new_second, new_cold, sq.reshape(width)


def solution(mesh):
    owned = P(("rep", "dp"), None)
    placed = (P("dp", "rep"), P("dp", None), P("dp", "rep", None), owned, owned, owned, P())
    return jax.shard_map(
        functools.partial(body, mesh.shape["dp"], mesh.shape["rep"]),
        mesh=mesh,
        in_specs=placed,
        out_specs=(owned, owned, owned, P("dp", "rep", None), P()),
        check_vma=False,
    )
```

profile of v0, /device:TPU:0, one launch (start us, length us, event | category | flops | bytes accessed | tf_op | source)
XLA Modules:
  0.0 105.5 jit_solution(8448028457647177529)
XLA Ops:
  0.6 0.0 copy-start
  0.6 2.2 %copy-done = bf16[1,2048,1024]{2,1,0:T(8,128)(2,1)S(1)} copy-done((bf16[1,2048,1024]{2,1,0:T(8,128)(2,1)S(1)}, bf16[1,2048,1024]{2,1,0:T(8,128)(2,1)}, u32[]{:S(2)}) %copy-start) | copy-done | bytes 4194328
  2.8 0.0 copy-start.1
  2.8 1.7 %copy-done.1 = bf16[640,2048]{1,0:T(8,128)(2,1)S(1)} copy-done((bf16[640,2048]{1,0:T(8,128)(2,1)S(1)}, bf16[640,2048]{1,0:T(8,128)(2,1)}, u32[]{:S(2)}) %copy-start.1) | copy-done | bytes 2621464
  4.6 0.0 copy-start.2
  4.6 1.3 %copy-done.2 = bf16[640,1024]{1,0:T(8,128)(2,1)S(1)} copy-done((bf16[640,1024]{1,0:T(8,128)(2,1)S(1)}, bf16[640,1024]{1,0:T(8,128)(2,1)}, u32[]{:S(2)}) %copy-start.2) | copy-done | bytes 1310744
  5.9 0.0 copy-start.3
  5.9 1.2 %copy-done.3 = f32[256,1024]{1,0:T(8,128)S(1)} copy-done((f32[256,1024]{1,0:T(8,128)S(1)}, f32[256,1024]{1,0:T(8,128)}, u32[]{:S(2)}) %copy-start.3) | copy-done | bytes 1048600
  7.1 0.0 copy-start.4
  7.1 1.2 %copy-done.4 = f32[256,1024]{1,0:T(8,128)S(1)} copy-done((f32[256,1024]{1,0:T(8,128)S(1)}, f32[256,1024]{1,0:T(8,128)}, u32[]{:S(2)}) %copy-start.4) | copy-done | bytes 1048600
  8.3 0.0 copy-start.5
  8.3 1.2 %copy-done.5 = f32[256,1024]{1,0:T(8,128)S(1)} copy-done((f32[256,1024]{1,0:T(8,128)S(1)}, f32[256,1024]{1,0:T(8,128)}, u32[]{:S(2)}) %copy-start.5) | copy-done | bytes 1048600
  9.6 0.0 copy-start.6
  9.6 0.7 copy-done.6
  10.2 91.1 %exchange.1 = (f32[256,512]{1,0:T(8,128)S(1)}, f32[8,128]{1,0:T(8,128)S(1)}, bf16[1,2048,1024]{2,1,0:T(8,128)(2,1)S(1)}, f32[256,1024]{1,0:T(8,128)S(1)}, f32[25...) custom-call(s32[8]{0:T(128)S(1)} %copy-done.6, bf16[640,2048]{1,0:T(8,128)(2,1)S(1)} %copy-done.1, ...), custom_call_target="tpu_custom_call" | custom-call | tf_op jit(solution)/shard_map/exchange/pallas_call | solution.py:331
  101.4 3.6 %update.1 = (f32[256,1024]{1,0:T(8,128)}, f32[256,1024]{1,0:T(8,128)}, f32[256,1024]{1,0:T(8,128)}, bf16[1,2048,1024]{2,1,0:T(8,128)(2,1)}) custom-call(s32[8]{0:T(128)S(1)} %copy-done.6, f32[256,512]{1,0:T(8,128)S(1)} %get-tuple-element.15.summed, f32[8,128]{1,0:T(8,128)S(1)} %get-tuple-element.16.sq, bf16[1,2048,1024]{2,1,0:T(8,128)(2,1)S(1)} %get-tuple-element.17.nc, ...), custom_call_target="tpu_custom_call" | custom-call | tf_op jit(solution)/shard_map/update/pallas_call | solution.py:369
  104.9 0.6 copy.13
Async XLA Ops:
  0.6 2.2 %copy-start = (bf16[1,2048,1024]{2,1,0:T(8,128)(2,1)S(1)}, bf16[1,2048,1024]{2,1,0:T(8,128)(2,1)}, u32[]{:S(2)}) copy-start(bf16[1,2048,1024]{2,1,0:T(8,128)(2,1)} %cold.1) | copy-start | bytes 12582916
  2.8 1.7 %copy-start.1 = (bf16[640,2048]{1,0:T(8,128)(2,1)S(1)}, bf16[640,2048]{1,0:T(8,128)(2,1)}, u32[]{:S(2)}) copy-start(bf16[640,2048]{1,0:T(8,128)(2,1)} %feat.1) | copy-start | bytes 7864324
  4.6 1.3 %copy-start.2 = (bf16[640,1024]{1,0:T(8,128)(2,1)S(1)}, bf16[640,1024]{1,0:T(8,128)(2,1)}, u32[]{:S(2)}) copy-start(bf16[640,1024]{1,0:T(8,128)(2,1)} %og.1) | copy-start | bytes 3932164
  5.9 1.2 %copy-start.3 = (f32[256,1024]{1,0:T(8,128)S(1)}, f32[256,1024]{1,0:T(8,128)}, u32[]{:S(2)}) copy-start(f32[256,1024]{1,0:T(8,128)} %weight.1) | copy-start | bytes 3145732
  7.1 1.2 %copy-start.4 = (f32[256,1024]{1,0:T(8,128)S(1)}, f32[256,1024]{1,0:T(8,128)}, u32[]{:S(2)}) copy-start(f32[256,1024]{1,0:T(8,128)} %moment.1) | copy-start | bytes 3145732
  8.3 1.2 %copy-start.5 = (f32[256,1024]{1,0:T(8,128)S(1)}, f32[256,1024]{1,0:T(8,128)}, u32[]{:S(2)}) copy-start(f32[256,1024]{1,0:T(8,128)} %second.1) | copy-start | bytes 3145732
  9.6 0.7 copy-start.6
where the time goes:
time: 106 us
  Pallas kernels  94.7 us (89%)
  local copies, waits for them, and re-layouts  10.2 us (10%)
    pallas_call x1, Pallas kernels, body(): pl.pallas_call(functools.partial(exchange_kernel, n, reps, hot), out_shap...  91.1 us
    unnamed x15, local copies, waits for them, and re-layouts  10.2 us
    pallas_call x1, Pallas kernels, body(): pl.pallas_call(functools.partial(update_kernel, n, rows * reps, tokens, h...  3.56 us

commit v1 on v0

v1 whole, which is shorter than its diff:
```python
import functools
import jax
import jax.numpy as jnp
from jax import lax
from jax.experimental import pallas as pl
from jax.experimental.pallas import tpu as pltpu
from jax.sharding import PartitionSpec as P

LANES = 128
FRONT = 5
VMEM_GRANT = 57 * 2**20
MESH = pl.DeviceIdType.MESH


def split_of(own):
    line = 8 * max(round(own / 48), 1)
    cross = own - line
    pieces = next(s for s in (3, 2, 1) if cross % (8 * s) == 0)
    return cross, line, pieces


def block_of(ranks, blocks, rank):
    found = 0
    for b in range(blocks):
        gap = ranks[b] - rank
        found = found + b * (1 - jnp.minimum(gap * gap, 1))
    return pl.multiple_of(found * LANES, LANES)


def exchange_kernel(
    n, reps, hot,
    ranks, feat, og, cold, weight, moment, second,
    summed, sq_out, kept, w_out, m_out, s_out,
    feat_v, og_v, og_p, cold_v, pack_a, pack_b, rx_a, rx_b, la, ra, lb, rb, sq, reps_sq, dp_sq,
    in_sem, state_sem, x_send, x_recv, za_send, la_recv, ra_recv, zb_send, lb_recv, rb_recv,
    b_send, b_recv, n1_send, n1_recv, n2_send, n2_recv,
):
    m = n // 2
    tokens = feat.shape[0]
    rows, width = cold.shape[1], cold.shape[2]
    blocks = width // LANES
    packed = hot * LANES
    own = rows // n
    chunk = max(own, LANES)
    chunks = rows // chunk
    inner = chunk // own
    cross_rows, line_rows, pieces = split_of(own)
    part = cross_rows // pieces
    me = lax.axis_index("dp")
    rep = lax.axis_index("rep")
    x = me % 2
    p = me // 2
    partner = me + 1 - 2 * x

    half = max(m // 2, 1)
    flip = p // half if m > 1 else 0
    pr = p + flip * (m - 1 - 2 * p)
    lone = m - 1 - 2 * pr

    def dest(k):
        late = (k - lone + 2 * m) // (2 * m)
        pair = late * (k - lone)
        odd = pair % 2
        near = (1 - late) * (m - 1 - k) + late * ((1 - odd) * (pair // 2) + odd * (2 * pr - pair // 2))
        return near + flip * (m - 1 - 2 * near)

    def chunk_at(i):
        if chunk != own:
            return i
        side = i % 2
        return 2 * dest(i // 2) + (1 - side) * (1 - x) + side * x

    def loop(count, step):
        if count <= 8:
            for k in range(count):
                step(k)
        else:
            def walk(k, carry):
                step(k)
                return carry

            lax.fori_loop(0, count, walk, 0)

    def rolled(count, step):
        def walk(k, carry):
            step(k)
            return carry

        lax.fori_loop(0, count, walk, 0)

    barrier = pltpu.get_barrier_semaphore()

    def peers(count, step):
        if count <= 8:
            for t in range(1, count):
                step(t)
        else:
            def walk(t, carry):
                step(t)
                return carry

            lax.fori_loop(1, count, walk, 0)

    peers(n, lambda t: pl.semaphore_signal(
        barrier, inc=1, device_id={"dp": (me + t) % n}, device_id_type=MESH))
    peers(reps, lambda t: pl.semaphore_signal(
        barrier, inc=1, device_id={"rep": (rep + t) % reps}, device_id_type=MESH))

    def feat_copy(i):
        cols = pl.ds(pl.multiple_of(chunk_at(i) * chunk, LANES), chunk)
        return pltpu.make_async_copy(feat.at[:, cols], feat_v.at[i], in_sem.at[0, i])

    def cold_copy(i):
        at = pl.ds(pl.multiple_of(chunk_at(i) * chunk, LANES), chunk)
        return pltpu.make_async_copy(cold.at[0, at], cold_v.at[i], in_sem.at[1, i])

    state = [
        pltpu.make_async_copy(src, dst, state_sem.at[i])
        for i, (src, dst) in enumerate(
            ((weight, w_out), (moment, m_out), (second, s_out), (og, og_v))
        )
    ]
    state[3].start()

    def fetch(i):
        feat_copy(i).start()
        cold_copy(i).start()

    rolled(chunks, fetch)
    for copy in state[:3]:
        copy.start()

    sq[...] = jnp.zeros_like(sq)
    picks = []
    for r in range(blocks):
        row = []
        for b in range(blocks):
            gap = ranks[b] - r
            row.append((1 - jnp.minimum(gap * gap, 1)).astype(jnp.float32))
        picks.append(row)

    def ranked(ref, index, r):
        held = None
        for b in range(blocks):
            part_b = ref[index + (slice(b * LANES, (b + 1) * LANES),)]
            part_b = part_b * jnp.full(part_b.shape, picks[r][b]).astype(part_b.dtype)
            held = part_b if held is None else held + part_b
        return held

    def cross(k, sub):
        d = dest(k)
        at = pl.ds(pl.multiple_of(sub * part, 8), part)
        return pltpu.make_async_remote_copy(
            src_ref=pack_a.at[2 * d + 1 - x, at], dst_ref=rx_a.at[d, at],
            send_sem=x_send.at[d, sub], recv_sem=x_recv.at[d, sub],
            device_id={"dp": partner}, device_id_type=MESH,
        )

    def along_a(d, sub, right):
        at = pl.ds(pl.multiple_of(sub * part, 8), part)
        return pltpu.make_async_remote_copy(
            src_ref=pack_a.at[2 * d + x, at], dst_ref=(la if right else ra).at[d, at],
            send_sem=za_send.at[d, sub], recv_sem=(la_recv if right else ra_recv).at[d, sub],
            device_id={"dp": me + 2 if right else me - 2}, device_id_type=MESH,
        )

    def along_b(d, right):
        return pltpu.make_async_remote_copy(
            src_ref=pack_b.at[d], dst_ref=(lb if right else rb).at[d],
            send_sem=zb_send.at[d], recv_sem=(lb_recv if right else rb_recv).at[d],
            device_id={"dp": me + 2 if right else me - 2}, device_id_type=MESH,
        )

    def cross_b():
        return pltpu.make_async_remote_copy(
            src_ref=pack_b.at[p, pl.ds(pl.multiple_of((1 - x) * line_rows, 8), line_rows)],
            dst_ref=rx_b, send_sem=b_send, recv_sem=b_recv,
            device_id={"dp": partner}, device_id_type=MESH,
        )

    def norm_rep(t):
        return pltpu.make_async_remote_copy(
            src_ref=sq, dst_ref=reps_sq.at[rep],
            send_sem=n1_send.at[t], recv_sem=n1_recv.at[rep],
            device_id={"rep": (rep + t) % reps}, device_id_type=MESH,
        )

    def norm_rep_in(t):
        j = (rep + t) % reps
        return pltpu.make_async_remote_copy(
            src_ref=sq, dst_ref=reps_sq.at[j],
            send_sem=n1_send.at[t], recv_sem=n1_recv.at[j],
            device_id={"rep": j}, device_id_type=MESH,
        )

    def norm_dp(t):
        return pltpu.make_async_remote_copy(
            src_ref=dp_sq.at[me], dst_ref=dp_sq.at[me],
            send_sem=n2_send.at[t], recv_sem=n2_recv.at[me],
            device_id={"dp": (me + t) % n}, device_id_type=MESH,
        )

    def norm_dp_in(t):
        j = (me + t) % n
        return pltpu.make_async_remote_copy(
            src_ref=dp_sq.at[j], dst_ref=dp_sq.at[j],
            send_sem=n2_send.at[t], recv_sem=n2_recv.at[j],
            device_id={"dp": j}, device_id_type=MESH,
        )

    def raw_b(k):
        d = dest(k)

        @pl.when(jnp.logical_and(d > p, p == 0))
        def _():
            along_b(d, True).start()

        @pl.when(jnp.logical_and(d < p, p == m - 1))
        def _():
            along_b(d, False).start()

    state[3].wait()
    for r in range(blocks):
        og_p[:, r * LANES:(r + 1) * LANES] = ranked(og_v, (slice(None),), r)
    pl.semaphore_wait(barrier, (n - 1) + (reps - 1))

    def product(i, lo, hi):
        grad = lax.dot_general(
            feat_v[i], og_p[:, lo * LANES:hi * LANES], (((0,), (0,)), ((), ())),
            preferred_element_type=jnp.float32,
        )
        pairs = []
        for r in range(lo, hi):
            held = ranked(cold_v, (i, slice(None)), r).astype(jnp.float32)
            value = grad[:, (r - lo) * LANES:(r - lo + 1) * LANES] + held
            sq[r:r + 1, :] += jnp.sum(value * value, axis=0, keepdims=True)
            pairs.append((r, value))
        return pairs

    def hot_step(i):
        feat_copy(i).wait()
        cold_copy(i).wait()
        c = chunk_at(i)
        for r, value in product(i, 0, hot):
            cols = slice(r * LANES, (r + 1) * LANES)
            for j in range(inner):
                owner = c * inner + j
                q, s = owner // 2, owner % 2
                pack_a[owner, :, cols] = value[j * own:j * own + cross_rows]
                pack_b[q, pl.ds(pl.multiple_of(s * line_rows, 8), line_rows), cols] = (
                    value[j * own + cross_rows:(j + 1) * own])
        if chunk == own:
            k = i // 2
            for sub in range(pieces):
                @pl.when(jnp.logical_and(i % 2 == 0, k * pieces + sub < FRONT))
                def _():
                    cross(k, sub).start()

            @pl.when(i % 2 == 1)
            def _():
                raw_b(k)

    def cold_step(i):
        at = pl.ds(pl.multiple_of(chunk_at(i) * chunk, LANES), chunk)
        for r, value in product(i, hot, blocks):
            cols = slice((r - hot) * LANES, (r - hot + 1) * LANES)
            kept[at, cols] = value.astype(jnp.bfloat16)

    rolled(chunks, hot_step)
    rolled(chunks, cold_step)
    if chunk != own:
        def launch(k):
            for sub in range(pieces):
                @pl.when(k * pieces + sub < FRONT)
                def _():
                    cross(k, sub).start()
            raw_b(k)

        rolled(m, launch)
    peers(reps, lambda t: norm_rep(t).start())

    def line_step(k):
        d = dest(k)

        @pl.when(jnp.logical_and(d >= p, p > 0))
        def _():
            along_b(d, True).wait_recv()
            pack_b[d] += lb[d]

        @pl.when(jnp.logical_and(d <= p, p < m - 1))
        def _():
            along_b(d, False).wait_recv()
            pack_b[d] += rb[d]

        @pl.when(jnp.logical_and(d > p, p > 0))
        def _():
            along_b(d, True).start()

        @pl.when(jnp.logical_and(d < p, p < m - 1))
        def _():
            along_b(d, False).start()

    peers(reps, lambda t: norm_rep_in(t).wait_recv())
    reps_sq[rep] = sq[...]
    total = reps_sq[0]
    for j in range(1, reps):
        total = total + reps_sq[j]
    dp_sq[me] = total
    peers(n, lambda t: norm_dp(t).start())

    def rest(k):
        for sub in range(pieces):
            @pl.when(k * pieces + sub >= FRONT)
            def _():
                cross(k, sub).start()

    rolled(m, rest)
    loop(m, line_step)
    cross_b().start()

    def cross_step(k):
        d = dest(k)
        for sub in range(pieces):
            at = slice(sub * part, (sub + 1) * part)
            cross(k, sub).wait_recv()
            pack_a[2 * d + x, at] += rx_a[d, at]

            @pl.when(jnp.logical_and(d >= p, p > 0))
            def _():
                along_a(d, sub, True).wait_recv()
                pack_a[2 * d + x, at] += la[d, at]

            @pl.when(jnp.logical_and(d <= p, p < m - 1))
            def _():
                along_a(d, sub, False).wait_recv()
                pack_a[2 * d + x, at] += ra[d, at]

            @pl.when(d > p)
            def _():
                along_a(d, sub, True).start()

            @pl.when(d < p)
            def _():
                along_a(d, sub, False).start()

            @pl.when(d == p)
            def _():
                summed[at] = pack_a[2 * d + x, at]

    loop(m - 1, cross_step)
    peers(n, lambda t: norm_dp_in(t).wait_recv())
    everything = dp_sq[0]
    for j in range(1, n):
        everything = everything + dp_sq[j]
    sq_out[...] = everything
    for copy in state[:3]:
        copy.wait()
    cross_b().wait_recv()
    mine = pl.ds(pl.multiple_of(x * line_rows, 8), line_rows)
    summed[cross_rows:] = pack_b[p, mine] + rx_b[...]
    cross_step(m - 1)

    def drain(k):
        d = dest(k)
        for sub in range(pieces):
            cross(k, sub).wait_send()

        @pl.when(d > p)
        def _():
            along_b(d, True).wait_send()
            for sub in range(pieces):
                along_a(d, sub, True).wait_send()

        @pl.when(d < p)
        def _():
            along_b(d, False).wait_send()
            for sub in range(pieces):
                along_a(d, sub, False).wait_send()

    rolled(m, drain)
    cross_b().wait_send()
    peers(reps, lambda t: norm_rep(t).wait_send())
    peers(n, lambda t: norm_dp(t).wait_send())


def update_kernel(
    n, total_rows, tokens, hot,
    ranks, summed, sq, kept, weight, moment, second,
    w_hbm, m_hbm, s_hbm, nc_hbm, sq_hbm,
    fresh, none, sq_v, nc_sem, state_sem, sq_sem,
):
    width = weight.shape[1]
    blocks = width // LANES
    where = [pl.ds(block_of(ranks, blocks, r), LANES) for r in range(blocks)]
    outs = (w_hbm, m_hbm, s_hbm)
    copies = []

    def send(src, dst, sem):
        copies.append(pltpu.make_async_copy(src, dst, sem))
        copies[-1].start()

    for r in range(hot, blocks):
        cols = pl.ds((r - hot) * LANES, LANES)
        send(kept.at[:, cols], nc_hbm.at[0, :, where[r]], nc_sem.at[r])
        for i, src in enumerate((weight, moment, second)):
            send(src.at[:, where[r]], outs[i].at[:, where[r]], state_sem.at[i, r])
    none[...] = jnp.zeros_like(none)
    for r in range(hot):
        send(none, nc_hbm.at[0, :, where[r]], nc_sem.at[r])
    for b in range(blocks):
        sq_v[b:b + 1, :] = sq[pl.ds(ranks[b], 1), :]
    send(sq_v, sq_hbm, sq_sem)
    for r in range(hot):
        cols = slice(r * LANES, (r + 1) * LANES)
        rms = jnp.sqrt(sq[r:r + 1, :] / jnp.float32(total_rows * n * tokens))
        clip = 1.0 / jnp.maximum(jnp.float32(1.0), rms)
        grad = summed[:, cols] * clip / jnp.float32(n)
        moved = 0.9 * moment[:, where[r]] + 0.1 * grad
        squared = 0.95 * second[:, where[r]] + 0.05 * grad * grad
        fresh[1, :, cols] = moved
        fresh[2, :, cols] = squared
        step = 0.05 * (moved / (1.0 - 0.9**10)) / (
            jnp.sqrt(squared / (1.0 - 0.95**10)) + 1e-08
        )
        fresh[0, :, cols] = weight[:, where[r]] - step
        for i in range(3):
            send(fresh.at[i, :, pl.ds(r * LANES, LANES)], outs[i].at[:, where[r]], state_sem.at[i, r])
    for copy in copies:
        copy.wait()


def body(n, reps, features, out_grads, cold_sums, weight, moment, second, ranks):
    tokens, rows = features.shape
    width = out_grads.shape[1]
    blocks = ranks.shape[0]
    hot = blocks // 2
    packed = hot * LANES
    m = n // 2
    own = rows // n
    chunk = max(own, LANES)
    chunks = rows // chunk
    cross_rows, line_rows, pieces = split_of(own)
    f32, bf16 = jnp.float32, jnp.bfloat16
    vmem = pl.BlockSpec(memory_space=pltpu.VMEM)
    smem = pl.BlockSpec(memory_space=pltpu.SMEM)
    hbm = pl.BlockSpec(memory_space=pl.ANY)
    dma = pltpu.SemaphoreType.DMA
    summed, sq, kept, w, mo, se = pl.pallas_call(
        functools.partial(exchange_kernel, n, reps, hot),
        out_shape=(
            pltpu.VMEM((own, packed), f32),
            pltpu.VMEM((blocks, LANES), f32),
            pltpu.VMEM((rows, width - packed), bf16),
            pltpu.VMEM(weight.shape, f32),
            pltpu.VMEM(weight.shape, f32),
            pltpu.VMEM(weight.shape, f32),
        ),
        in_specs=[smem] + [pl.BlockSpec(memory_space=pltpu.HBM)] * 6,
        out_specs=(vmem,) * 6,
        scratch_shapes=[
            pltpu.VMEM((chunks, tokens, chunk), bf16),
            pltpu.VMEM((tokens, width), bf16),
            pltpu.VMEM((tokens, width), bf16),
            pltpu.VMEM((chunks, chunk, width), bf16),
            pltpu.VMEM((n, cross_rows, packed), f32),
            pltpu.VMEM((m, 2 * line_rows, packed), f32),
            pltpu.VMEM((m, cross_rows, packed), f32),
            pltpu.VMEM((line_rows, packed), f32),
            pltpu.VMEM((m, cross_rows, packed), f32),
            pltpu.VMEM((m, cross_rows, packed), f32),
            pltpu.VMEM((m, 2 * line_rows, packed), f32),
            pltpu.VMEM((m, 2 * line_rows, packed), f32),
            pltpu.VMEM((blocks, LANES), f32),
            pltpu.VMEM((reps, blocks, LANES), f32),
            pltpu.VMEM((n, blocks, LANES), f32),
            dma((2, chunks)),
            dma((4,)),
            dma((m, pieces)),
            dma((m, pieces)),
            dma((m, pieces)),
            dma((m, pieces)),
            dma((m, pieces)),
            dma((m,)),
            dma((m,)),
            dma((m,)),
            dma,
            dma,
            dma((reps,)),
            dma((reps,)),
            dma((n,)),
            dma((n,)),
        ],
        compiler_params=pltpu.CompilerParams(
            collective_id=0, has_side_effects=True, vmem_limit_bytes=VMEM_GRANT
        ),
        name="exchange",
    )(ranks, features, out_grads, cold_sums, weight, moment, second)
    new_weight, new_moment, new_second, new_cold, column_sq = pl.pallas_call(
        functools.partial(update_kernel, n, rows * reps, tokens, hot),
        out_shape=(
            jax.ShapeDtypeStruct(weight.shape, f32),
            jax.ShapeDtypeStruct(weight.shape, f32),
            jax.ShapeDtypeStruct(weight.shape, f32),
            jax.ShapeDtypeStruct(cold_sums.shape, bf16),
            jax.ShapeDtypeStruct((blocks, LANES), f32),
        ),
        in_specs=[smem] + [vmem] * 6,
        out_specs=(hbm,) * 5,
        scratch_shapes=[
            pltpu.VMEM((3, weight.shape[0], packed), f32),
            pltpu.VMEM((rows, LANES), bf16),
            pltpu.VMEM((blocks, LANES), f32),
            dma((blocks,)),
            dma((3, blocks)),
            dma,
        ],
        compiler_params=pltpu.CompilerParams(vmem_limit_bytes=VMEM_GRANT // 2),
        name="update",
    )(ranks, summed, sq, kept, w, mo, se)
    return new_weight, new_moment, new_second, new_cold, column_sq.reshape(width)


def solution(mesh):
    owned = P(("rep", "dp"), None)
    placed = (P("dp", "rep"), P("dp", None), P("dp", "rep", None), owned, owned, owned, P())
    return jax.shard_map(
        functools.partial(body, mesh.shape["dp"], mesh.shape["rep"]),
        mesh=mesh,
        in_specs=placed,
        out_specs=(owned, owned, owned, P("dp", "rep", None), P()),
        check_vma=False,
    )
```

time: 106 us -> 64.1 us (0.60)
  Pallas kernels: 94.7 us -> 63.3 us
  local copies, waits for them, and re-layouts: 10.2 us -> 0.01 us
    pallas_call x1, Pallas kernels: 91.1 us -> 59.5 us  [body(): pl.pallas_call(functools.partial(exchange_kernel, n, reps, hot), out_shap...]
    unnamed x15 -> x2, local copies, waits for them, and re-layouts: 10.2 us -> 0.01 us
where the time goes in v1:
time: 64.1 us; the launch traced here: 64 us
  Pallas kernels  63.3 us (99%)
  between operations  0.66 us (1%)
    pallas_call x1, Pallas kernels, body(): pl.pallas_call(functools.partial(exchange_kernel, n, reps, hot), out_shap...  59.5 us
    pallas_call x1, Pallas kernels, body(): pl.pallas_call(functools.partial(update_kernel, n, rows * reps, tokens, h...  3.82 us

profile of v1, /device:TPU:0, one launch (start us, length us, event | category | flops | bytes accessed | tf_op | source)
XLA Modules:
  0.0 64.0 jit_solution(17949543856965641418)
XLA Ops:
  0.6 0.0 copy-start
  0.6 59.5 %exchange.1 = (f32[256,512]{1,0:T(8,128)S(1)}, f32[8,128]{1,0:T(8,128)S(1)}, bf16[2048,512]{1,0:T(8,128)(2,1)S(1)}, f32[256,1024]{1,0:T(8,128)S(1)}, f32[256,1024]{1,0:T(8,128)S(1)}, /*index=5*/f32[256,1024]{1,0:T(8,128)S(1)}) custom-call(s32[8]{0:T(128)} %ranks.3, bf16[640,2048]{1,0:T(8,128)(2,1)} %feat.1, bf16[640,1024]{1,0:T(8,128)(2,1)} %og.1, ...), custom_call_target="tpu_custom_call" | custom-call | tf_op jit(solution)/shard_map/exchange/pallas_call | solution.py:448
  60.2 0.0 copy-done
  60.2 3.8 %update.1 = (f32[256,1024]{1,0:T(8,128)}, f32[256,1024]{1,0:T(8,128)}, f32[256,1024]{1,0:T(8,128)}, bf16[1,2048,1024]{2,1,0:T(8,128)(2,1)}, f32[8,128]{1,0:T(8,128)}) custom-call(s32[8]{0:T(128)S(1)} %copy-done, f32[256,512]{1,0:T(8,128)S(1)} %get-tuple-element.16.summed, f32[8,128]{1,0:T(8,128)S(1)} %get-tuple-element.17.sq, ...), custom_call_target="tpu_custom_call" | custom-call | tf_op jit(solution)/shard_map/update/pallas_call | solution.py:498
Async XLA Ops:
  0.6 59.5 %copy-start = (s32[8]{0:T(128)S(1)}, s32[8]{0:T(128)}, u32[]{:S(2)}) copy-start(s32[8]{0:T(128)} %ranks.3) | copy-start | bytes 100

commit v2 on v1

--- a/solution.py
+++ b/solution.py
@@ -7,7 +7,7 @@
 from jax.sharding import PartitionSpec as P
 
 LANES = 128
-FRONT = 5
+FRONT = 9
 VMEM_GRANT = 57 * 2**20
 MESH = pl.DeviceIdType.MESH
 
@@ -70,41 +70,17 @@
         side = i % 2
         return 2 * dest(i // 2) + (1 - side) * (1 - x) + side * x
 
-    def loop(count, step):
-        if count <= 8:
-            for k in range(count):
+    def span(lo, hi, step):
+        if hi - lo <= 8:
+            for k in range(lo, hi):
                 step(k)
         else:
-            def walk(k, carry):
-                step(k)
-                return carry
-
-            lax.fori_loop(0, count, walk, 0)
-
-    def rolled(count, step):
-        def walk(k, carry):
-            step(k)
-            return carry
-
-        lax.fori_loop(0, count, walk, 0)
+            lax.fori_loop(lo, hi, lambda k, carry: step(k) or carry, 0)
+
+    def rolled(lo, hi, step):
+        lax.fori_loop(lo, hi, lambda k, carry: step(k) or carry, 0)
 
     barrier = pltpu.get_barrier_semaphore()
-
-    def peers(count, step):
-        if count <= 8:
-            for t in range(1, count):
-                step(t)
-        else:
-            def walk(t, carry):
-                step(t)
-                return carry
-
-            lax.fori_loop(1, count, walk, 0)
-
-    peers(n, lambda t: pl.semaphore_signal(
-        barrier, inc=1, device_id={"dp": (me + t) % n}, device_id_type=MESH))
-    peers(reps, lambda t: pl.semaphore_signal(
-        barrier, inc=1, device_id={"rep": (rep + t) % reps}, device_id_type=MESH))
 
     def feat_copy(i):
         cols = pl.ds(pl.multiple_of(chunk_at(i) * chunk, LANES), chunk)
@@ -120,15 +96,17 @@
             ((weight, w_out), (moment, m_out), (second, s_out), (og, og_v))
         )
     ]
-    state[3].start()
-
     def fetch(i):
         feat_copy(i).start()
         cold_copy(i).start()
 
-    rolled(chunks, fetch)
-    for copy in state[:3]:
-        copy.start()
+    state[3].start()
+    fetch(0)
+    span(1, n, lambda t: pl.semaphore_signal(
+        barrier, inc=1, device_id={"dp": (me + t) % n}, device_id_type=MESH))
+    span(1, reps, lambda t: pl.semaphore_signal(
+        barrier, inc=1, device_id={"rep": (rep + t) % reps}, device_id_type=MESH))
+    rolled(1, chunks, fetch)
 
     sq[...] = jnp.zeros_like(sq)
     picks = []
@@ -220,7 +198,7 @@
             along_b(d, False).start()
 
     state[3].wait()
-    for r in range(blocks):
+    for r in range(hot):
         og_p[:, r * LANES:(r + 1) * LANES] = ranked(og_v, (slice(None),), r)
     pl.semaphore_wait(barrier, (n - 1) + (reps - 1))
 
@@ -266,8 +244,12 @@
             cols = slice((r - hot) * LANES, (r - hot + 1) * LANES)
             kept[at, cols] = value.astype(jnp.bfloat16)
 
-    rolled(chunks, hot_step)
-    rolled(chunks, cold_step)
+    rolled(0, chunks, hot_step)
+    for copy in state[:3]:
+        copy.start()
+    for r in range(hot, blocks):
+        og_p[:, r * LANES:(r + 1) * LANES] = ranked(og_v, (slice(None),), r)
+    rolled(0, chunks, cold_step)
     if chunk != own:
         def launch(k):
             for sub in range(pieces):
@@ -276,8 +258,8 @@
                     cross(k, sub).start()
             raw_b(k)
 
-        rolled(m, launch)
-    peers(reps, lambda t: norm_rep(t).start())
+        rolled(0, m, launch)
+    span(1, reps, lambda t: norm_rep(t).start())
 
     def line_step(k):
         d = dest(k)
@@ -299,24 +281,12 @@
         @pl.when(jnp.logical_and(d < p, p < m - 1))
         def _():
             along_b(d, False).start()
-
-    peers(reps, lambda t: norm_rep_in(t).wait_recv())
-    reps_sq[rep] = sq[...]
-    total = reps_sq[0]
-    for j in range(1, reps):
-        total = total + reps_sq[j]
-    dp_sq[me] = total
-    peers(n, lambda t: norm_dp(t).start())
 
     def rest(k):
         for sub in range(pieces):
             @pl.when(k * pieces + sub >= FRONT)
             def _():
                 cross(k, sub).start()
-
-    rolled(m, rest)
-    loop(m, line_step)
-    cross_b().start()
 
     def cross_step(k):
         d = dest(k)
@@ -347,18 +317,33 @@
             def _():
                 summed[at] = pack_a[2 * d + x, at]
 
-    loop(m - 1, cross_step)
-    peers(n, lambda t: norm_dp_in(t).wait_recv())
+    span(0, m - 1, line_step)
+    if m > 1:
+        cross_step(0)
+    span(1, reps, lambda t: norm_rep_in(t).wait_recv())
+    reps_sq[rep] = sq[...]
+    total = reps_sq[0]
+    for j in range(1, reps):
+        total = total + reps_sq[j]
+    dp_sq[me] = total
+    span(1, n, lambda t: norm_dp(t).start())
+    rolled(0, m, rest)
+    span(1, m - 2, cross_step)
+    line_step(m - 1)
+    cross_b().start()
+    if m > 2:
+        cross_step(m - 2)
+    span(1, n, lambda t: norm_dp_in(t).wait_recv())
     everything = dp_sq[0]
     for j in range(1, n):
         everything = everything + dp_sq[j]
     sq_out[...] = everything
     for copy in state[:3]:
         copy.wait()
+    cross_step(m - 1)
     cross_b().wait_recv()
     mine = pl.ds(pl.multiple_of(x * line_rows, 8), line_rows)
     summed[cross_rows:] = pack_b[p, mine] + rx_b[...]
-    cross_step(m - 1)
 
     def drain(k):
         d = dest(k)
@@ -377,10 +362,10 @@
             for sub in range(pieces):
                 along_a(d, sub, False).wait_send()
 
-    rolled(m, drain)
+    rolled(0, m, drain)
     cross_b().wait_send()
-    peers(reps, lambda t: norm_rep(t).wait_send())
-    peers(n, lambda t: norm_dp(t).wait_send())
+    span(1, reps, lambda t: norm_rep(t).wait_send())
+    span(1, n, lambda t: norm_dp(t).wait_send())
 
 
 def update_kernel(

time: 64.1 us -> 54.3 us (0.85)
  Pallas kernels: 63.3 us -> 53.5 us
    pallas_call x1, Pallas kernels: 59.5 us -> 49.6 us  [body(): pl.pallas_call(functools.partial(exchange_kernel, n, reps, hot), out_shap...]
where the time goes in v2:
time: 54.3 us; the launch traced here: 54.1 us
  Pallas kernels  53.5 us (99%)
  between operations  0.66 us (1%)
    pallas_call x1, Pallas kernels, body(): pl.pallas_call(functools.partial(exchange_kernel, n, reps, hot), out_shap...  49.6 us
    pallas_call x1, Pallas kernels, body(): pl.pallas_call(functools.partial(update_kernel, n, rows * reps, tokens, h...  3.82 us

profile of v2, /device:TPU:0, one launch (start us, length us, event | category | flops | bytes accessed | tf_op | source)
XLA Modules:
  0.0 54.1 jit_solution(17470212514191747423)
XLA Ops:
  0.6 0.0 copy-start
  0.6 49.6 %exchange.1 = (f32[256,512]{1,0:T(8,128)S(1)}, f32[8,128]{1,0:T(8,128)S(1)}, bf16[2048,512]{1,0:T(8,128)(2,1)S(1)}, f32[256,1024]{1,0:T(8,128)S(1)}, f32[256,1024]{1,0:T(8,128)S(1)}, /*index=5*/f32[256,1024]{1,0:T(8,128)S(1)}) custom-call(s32[8]{0:T(128)} %ranks.3, bf16[640,2048]{1,0:T(8,128)(2,1)} %feat.1, bf16[640,1024]{1,0:T(8,128)(2,1)} %og.1, ...), custom_call_target="tpu_custom_call" | custom-call | tf_op jit(solution)/shard_map/exchange/pallas_call | solution.py:433
  50.3 0.0 copy-done
  50.3 3.8 %update.1 = (f32[256,1024]{1,0:T(8,128)}, f32[256,1024]{1,0:T(8,128)}, f32[256,1024]{1,0:T(8,128)}, bf16[1,2048,1024]{2,1,0:T(8,128)(2,1)}, f32[8,128]{1,0:T(8,128)}) custom-call(s32[8]{0:T(128)S(1)} %copy-done, f32[256,512]{1,0:T(8,128)S(1)} %get-tuple-element.16.summed, f32[8,128]{1,0:T(8,128)S(1)} %get-tuple-element.17.sq, ...), custom_call_target="tpu_custom_call" | custom-call | tf_op jit(solution)/shard_map/update/pallas_call | solution.py:483
Async XLA Ops:
  0.6 49.7 %copy-start = (s32[8]{0:T(128)S(1)}, s32[8]{0:T(128)}, u32[]{:S(2)}) copy-start(s32[8]{0:T(128)} %ranks.3) | copy-start | bytes 100

commit v3 on v2

v3 whole, which is shorter than its diff:
```python
import functools
import jax
import jax.numpy as jnp
from jax import lax
from jax.experimental import pallas as pl
from jax.experimental.pallas import tpu as pltpu
from jax.sharding import PartitionSpec as P

LANES = 128
GROUP = 32
FRONT = 6
VMEM_GRANT = 55 * 2**20
MESH = pl.DeviceIdType.MESH


def split_of(own):
    line = 8 * max(round(own / 48), 1)
    cross = own - line
    pieces = next(s for s in (3, 2, 1) if cross % (8 * s) == 0)
    return cross, line, pieces


def block_of(ranks, blocks, rank):
    found = 0
    for b in range(blocks):
        gap = ranks[b] - rank
        found = found + b * (1 - jnp.minimum(gap * gap, 1))
    return pl.multiple_of(found * LANES, LANES)


def exchange_kernel(
    n, reps, hot,
    ranks_hbm, feat, og, cold, weight, moment, second,
    summed, sq_out, kept, w_out, m_out, s_out,
    ranks, feat_v, og_v, og_p, cold_v, pack_a, pack_b, rx_a, rx_b, zin_a, zin_b, sq, reps_sq, pair_sq, line_sq,
    in_sem, state_sem, x_send, x_recv, za_send, za_recv, zb_send, zb_recv, b_send, b_recv,
    nr_send, nr_recv, nx_send, nx_recv, nz_send, nz_recv, from_left, from_right,
):
    m = n // 2
    tokens = feat.shape[0]
    rows, width = cold.shape[1], cold.shape[2]
    blocks = width // LANES
    packed = hot * LANES
    own = rows // n
    chunk = max(own, LANES)
    chunks = rows // chunk
    inner = chunk // own
    cross_rows, line_rows, pieces = split_of(own)
    part = cross_rows // pieces
    me = lax.axis_index("dp")
    rep = lax.axis_index("rep")
    x = me % 2
    p = me // 2
    partner = me + 1 - 2 * x

    half = max(m // 2, 1)
    flip = p // half if m > 1 else 0
    pr = p + flip * (m - 1 - 2 * p)
    lone = m - 1 - 2 * pr

    def dest(k):
        late = (k - lone + 2 * m) // (2 * m)
        pair = late * (k - lone)
        odd = pair % 2
        near = (1 - late) * (m - 1 - k) + late * ((1 - odd) * (pair // 2) + odd * (2 * pr - pair // 2))
        return near + flip * (m - 1 - 2 * near)

    def chunk_at(i):
        if chunk != own:
            return i
        side = i % 2
        return 2 * dest(i // 2) + (1 - side) * (1 - x) + side * x

    def span(lo, hi, step):
        if hi - lo <= 8:
            for k in range(lo, hi):
                step(k)
        else:
            lax.fori_loop(lo, hi, lambda k, carry: step(k) or carry, 0)

    def rolled(lo, hi, step):
        lax.fori_loop(lo, hi, lambda k, carry: step(k) or carry, 0)

    barrier = pltpu.get_barrier_semaphore()

    def feat_copy(i):
        cols = pl.ds(pl.multiple_of(chunk_at(i) * chunk, LANES), chunk)
        return pltpu.make_async_copy(feat.at[:, cols], feat_v.at[i], in_sem.at[0, i])

    def cold_copy(i):
        at = pl.ds(pl.multiple_of(chunk_at(i) * chunk, LANES), chunk)
        return pltpu.make_async_copy(cold.at[0, at], cold_v.at[i], in_sem.at[1, i])

    state = [
        pltpu.make_async_copy(src, dst, state_sem.at[i])
        for i, (src, dst) in enumerate(
            ((weight, w_out), (moment, m_out), (second, s_out), (og, og_v), (ranks_hbm, ranks))
        )
    ]
    def fetch(i):
        feat_copy(i).start()
        cold_copy(i).start()

    state[3].start()
    state[4].start()
    fetch(0)
    pl.semaphore_signal(barrier, inc=1, device_id={"dp": partner}, device_id_type=MESH)

    @pl.when(p > 0)
    def _():
        pl.semaphore_signal(barrier, inc=1, device_id={"dp": me - 2}, device_id_type=MESH)

    @pl.when(p < m - 1)
    def _():
        pl.semaphore_signal(barrier, inc=1, device_id={"dp": me + 2}, device_id_type=MESH)

    span(1, reps, lambda t: pl.semaphore_signal(
        barrier, inc=1, device_id={"rep": (rep + t) % reps}, device_id_type=MESH))
    rolled(1, chunks, fetch)

    sq[...] = jnp.zeros_like(sq)

    def ranked(load, lo, hi):
        parts = [load(slice(b * LANES, (b + 1) * LANES)) for b in range(blocks)]
        found = []
        for r in range(lo, hi):
            held = parts[0]
            for b in range(1, blocks):
                held = jnp.where(ranks[b] == r, parts[b], held)
            found.append(held)
        return found

    def cross(k, sub):
        d = dest(k)
        at = pl.ds(pl.multiple_of(sub * part, 8), part)
        return pltpu.make_async_remote_copy(
            src_ref=pack_a.at[2 * d + 1 - x, at], dst_ref=rx_a.at[d, at],
            send_sem=x_send, recv_sem=x_recv.at[d, sub],
            device_id={"dp": partner}, device_id_type=MESH,
        )

    def along_a(d, sub, right):
        at = pl.ds(pl.multiple_of(sub * part, 8), part)
        slot = d + 1 if right else d
        return pltpu.make_async_remote_copy(
            src_ref=pack_a.at[2 * d + x, at], dst_ref=zin_a.at[slot, at],
            send_sem=za_send, recv_sem=za_recv.at[slot, sub],
            device_id={"dp": me + 2 if right else me - 2}, device_id_type=MESH,
        )

    def along_b(d, right):
        slot = d + 1 if right else d
        return pltpu.make_async_remote_copy(
            src_ref=pack_b.at[d], dst_ref=zin_b.at[slot],
            send_sem=zb_send, recv_sem=zb_recv.at[slot],
            device_id={"dp": me + 2 if right else me - 2}, device_id_type=MESH,
        )

    def cross_b():
        return pltpu.make_async_remote_copy(
            src_ref=pack_b.at[p, pl.ds(pl.multiple_of((1 - x) * line_rows, 8), line_rows)],
            dst_ref=rx_b, send_sem=b_send, recv_sem=b_recv,
            device_id={"dp": partner}, device_id_type=MESH,
        )

    def norm_rep(t):
        return pltpu.make_async_remote_copy(
            src_ref=reps_sq.at[rep], dst_ref=reps_sq.at[rep], send_sem=nr_send, recv_sem=nr_recv,
            device_id={"rep": (rep + t) % reps}, device_id_type=MESH,
        )

    def norm_x():
        return pltpu.make_async_remote_copy(
            src_ref=pair_sq.at[x], dst_ref=pair_sq.at[x], send_sem=nx_send, recv_sem=nx_recv,
            device_id={"dp": partner}, device_id_type=MESH,
        )

    def norm_z(t):
        return pltpu.make_async_remote_copy(
            src_ref=line_sq.at[p], dst_ref=line_sq.at[p], send_sem=nz_send, recv_sem=nz_recv,
            device_id={"dp": 2 * ((p + t) % m) + x}, device_id_type=MESH,
        )

    def bytes_of(ref, send_sem, recv_sem):
        return pltpu.make_async_remote_copy(
            src_ref=ref, dst_ref=ref, send_sem=send_sem, recv_sem=recv_sem,
            device_id={"dp": partner}, device_id_type=MESH,
        )

    def token(right):
        pl.semaphore_signal(
            from_left if right else from_right, inc=1,
            device_id={"dp": me + 2 if right else me - 2}, device_id_type=MESH,
        )

    def raw_b(k):
        d = dest(k)

        @pl.when(jnp.logical_and(d > p, p == 0))
        def _():
            along_b(d, True).start()

        @pl.when(jnp.logical_and(d < p, p == m - 1))
        def _():
            along_b(d, False).start()

    def permute(lo, hi):
        for g in range(0, tokens, GROUP):
            at = slice(g, min(g + GROUP, tokens))
            for r, held in enumerate(ranked(lambda cols: og_v[at, cols], lo, hi), lo):
                og_p[at, r * LANES:(r + 1) * LANES] = held

    def product(i, lo, hi, store):
        grad = lax.dot_general(
            feat_v[i], og_p[:, lo * LANES:hi * LANES], (((0,), (0,)), ((), ())),
            preferred_element_type=jnp.float32,
        )
        squares = [sq[r] for r in range(lo, hi)]
        for g in range(0, chunk, GROUP):
            at = slice(g, g + GROUP)
            held = ranked(lambda cols: cold_v[i, at, cols], lo, hi)
            values = []
            for t in range(hi - lo):
                value = grad[at, t * LANES:(t + 1) * LANES] + held[t].astype(jnp.float32)
                for h in range(0, GROUP, 8):
                    squares[t] += value[h:h + 8] * value[h:h + 8]
                values.append(value)
            store(g, values)
        for r in range(lo, hi):
            sq[r] = squares[r - lo]

    def hot_fill(i):
        c = chunk_at(i)

        def store(g, values):
            for h in range(0, GROUP, 8):
                owner = c * inner + (g + h) // own
                row = (g + h) % own
                for r in range(hot):
                    cols = slice(r * LANES, (r + 1) * LANES)
                    if row < cross_rows:
                        pack_a[owner, row:row + 8, cols] = values[r][h:h + 8]
                    else:
                        at = pl.ds(pl.multiple_of((owner % 2) * line_rows + row - cross_rows, 8), 8)
                        pack_b[owner // 2, at, cols] = values[r][h:h + 8]

        product(i, 0, hot, store)

    def hot_step(i):
        feat_copy(i).wait()
        cold_copy(i).wait()
        hot_fill(i)
        if chunk == own:
            k = i // 2
            for sub in range(pieces):
                @pl.when(jnp.logical_and(i % 2 == 0, k * pieces + sub < FRONT))
                def _():
                    cross(k, sub).start()

            @pl.when(i % 2 == 1)
            def _():
                raw_b(k)

    def cold_step(i):
        c = chunk_at(i)

        def store(g, values):
            at = pl.ds(pl.multiple_of(c * chunk + g, 16), GROUP)
            values = [value.astype(jnp.bfloat16) for value in values]
            for b in range(blocks):
                new = jnp.zeros_like(values[0])
                for r in range(hot, blocks):
                    new = jnp.where(ranks[b] == r, values[r - hot], new)
                kept[at, b * LANES:(b + 1) * LANES] = new

        product(i, hot, blocks, store)

    state[4].wait()
    feat_copy(0).wait()
    cold_copy(0).wait()
    state[3].wait()
    permute(0, hot)
    hot_fill(0)
    greeted = (p + m - 1) // m + (2 * m - 2 - p) // m + 1 + (reps - 1)
    pl.semaphore_wait(barrier, greeted)

    @pl.when(jnp.logical_and(p == 0, m > 1))
    def _():
        token(True)

    @pl.when(jnp.logical_and(p == m - 1, m > 1))
    def _():
        token(False)

    if chunk == own:
        for sub in range(min(pieces, FRONT)):
            cross(0, sub).start()
    rolled(1, chunks, hot_step)
    for copy in state[:3]:
        copy.start()
    permute(hot, blocks)
    rolled(0, chunks, cold_step)
    if chunk != own:
        def launch(k):
            for sub in range(pieces):
                @pl.when(k * pieces + sub < FRONT)
                def _():
                    cross(k, sub).start()
            raw_b(k)

        rolled(0, m, launch)
    for r in range(blocks):
        reps_sq[rep, r:r + 1] = jnp.sum(sq[r], axis=0, keepdims=True)
    span(1, reps, lambda t: norm_rep(t).start())

    def line_step(k):
        d = dest(k)

        @pl.when(jnp.logical_and(d >= p, p > 0))
        def _():
            along_b(d, True).wait_recv()
            pack_b[d] += zin_b[d + 1]

        @pl.when(jnp.logical_and(d <= p, p < m - 1))
        def _():
            along_b(d, False).wait_recv()
            pack_b[d] += zin_b[d]

        @pl.when(jnp.logical_and(d > p, p > 0))
        def _():
            along_b(d, True).start()

        @pl.when(jnp.logical_and(d < p, p < m - 1))
        def _():
            along_b(d, False).start()

    def rest(k):
        for sub in range(pieces):
            @pl.when(k * pieces + sub >= FRONT)
            def _():
                cross(k, sub).start()

    def cross_step(k, subs=range(pieces)):
        d = dest(k)
        for sub in subs:
            at = slice(sub * part, (sub + 1) * part)
            cross(k, sub).wait_recv()
            pack_a[2 * d + x, at] += rx_a[d, at]

            @pl.when(jnp.logical_and(d >= p, p > 0))
            def _():
                along_a(d, sub, True).wait_recv()
                pack_a[2 * d + x, at] += zin_a[d + 1, at]

            @pl.when(jnp.logical_and(d <= p, p < m - 1))
            def _():
                along_a(d, sub, False).wait_recv()
                pack_a[2 * d + x, at] += zin_a[d, at]

            @pl.when(d > p)
            def _():
                along_a(d, sub, True).start()

            @pl.when(d < p)
            def _():
                along_a(d, sub, False).start()

            @pl.when(d == p)
            def _():
                summed[at] = pack_a[2 * d + x, at]

    span(0, m - 1, line_step)

    @pl.when(jnp.logical_and(p > 0, p < m - 1))
    def _():
        pl.semaphore_wait(from_right, 1)
        token(False)
        pl.semaphore_wait(from_left, 1)
        token(True)

    if m > 1:
        cross_step(0, range(1))
    bytes_of(reps_sq.at[pl.ds(0, reps - 1)], nr_send, nr_recv).wait_recv()
    total = reps_sq[0]
    for j in range(1, reps):
        total = total + reps_sq[j]
    pair_sq[x] = total
    norm_x().start()
    rolled(0, m, rest)
    if m > 1:
        cross_step(0, range(1, pieces))
    if m > 2:
        cross_step(1)
    norm_x().wait_recv()
    line_sq[p] = pair_sq[0] + pair_sq[1]

    @pl.when(jnp.logical_and(p == 0, m > 1))
    def _():
        pl.semaphore_wait(from_right, 1)

    @pl.when(jnp.logical_and(p == m - 1, m > 1))
    def _():
        pl.semaphore_wait(from_left, 1)

    span(1, m, lambda t: norm_z(t).start())
    span(2, m - 2, cross_step)
    line_step(m - 1)
    cross_b().start()
    if m > 3:
        cross_step(m - 2)
    if m > 1:
        bytes_of(line_sq.at[pl.ds(0, m - 1)], nz_send, nz_recv).wait_recv()
    everything = line_sq[0]
    for j in range(1, m):
        everything = everything + line_sq[j]
    sq_out[...] = everything
    for copy in state[:3]:
        copy.wait()
    cross_step(m - 1)
    cross_b().wait_recv()
    mine = pl.ds(pl.multiple_of(x * line_rows, 8), line_rows)
    summed[cross_rows:] = pack_b[p, mine] + rx_b[...]

    bytes_of(rx_a, x_send, x_recv.at[0, 0]).wait_send()
    if m > 1:
        bytes_of(zin_a.at[pl.ds(0, m - 1)], za_send, za_recv.at[0, 0]).wait_send()
        bytes_of(zin_b.at[pl.ds(0, m - 1)], zb_send, zb_recv.at[0]).wait_send()
        bytes_of(line_sq.at[pl.ds(0, m - 1)], nz_send, nz_recv).wait_send()
    cross_b().wait_send()
    norm_x().wait_send()
    bytes_of(reps_sq.at[pl.ds(0, reps - 1)], nr_send, nr_recv).wait_send()


def update_kernel(
    n, total_rows, tokens, hot,
    ranks_any, summed, sq, kept, weight, moment, second,
    w_hbm, m_hbm, s_hbm, nc_hbm, sq_hbm,
    ranks, fresh, sq_v, nc_sem, state_sem, sq_sem, ranks_sem,
):
    width = weight.shape[1]
    blocks = width // LANES
    outs = (w_hbm, m_hbm, s_hbm)
    copies = []

    def send(src, dst, sem):
        copies.append(pltpu.make_async_copy(src, dst, sem))
        copies[-1].start()

    order = pltpu.make_async_copy(ranks_any, ranks, ranks_sem)
    order.start()
    send(kept, nc_hbm.at[0], nc_sem)
    order.wait()
    where = [pl.ds(block_of(ranks, blocks, r), LANES) for r in range(blocks)]
    for r in range(hot, blocks):
        for i, src in enumerate((weight, moment, second)):
            send(src.at[:, where[r]], outs[i].at[:, where[r]], state_sem.at[i, r])
    for b in range(blocks):
        sq_v[b:b + 1, :] = sq[pl.ds(ranks[b], 1), :]
    send(sq_v, sq_hbm, sq_sem)
    for r in range(hot):
        cols = slice(r * LANES, (r + 1) * LANES)
        rms = jnp.sqrt(sq[r:r + 1, :] / jnp.float32(total_rows * n * tokens))
        clip = 1.0 / jnp.maximum(jnp.float32(1.0), rms)
        grad = summed[:, cols] * clip / jnp.float32(n)
        moved = 0.9 * moment[:, where[r]] + 0.1 * grad
        squared = 0.95 * second[:, where[r]] + 0.05 * grad * grad
        fresh[1, :, cols] = moved
        fresh[2, :, cols] = squared
        step = 0.05 * (moved / (1.0 - 0.9**10)) / (
            jnp.sqrt(squared / (1.0 - 0.95**10)) + 1e-08
        )
        fresh[0, :, cols] = weight[:, where[r]] - step
        for i in range(3):
            send(fresh.at[i, :, pl.ds(r * LANES, LANES)], outs[i].at[:, where[r]], state_sem.at[i, r])
    for copy in copies:
        copy.wait()


def body(n, reps, features, out_grads, cold_sums, weight, moment, second, ranks):
    tokens, rows = features.shape
    width = out_grads.shape[1]
    blocks = ranks.shape[0]
    hot = blocks // 2
    packed = hot * LANES
    m = n // 2
    own = rows // n
    chunk = max(own, LANES)
    chunks = rows // chunk
    cross_rows, line_rows, pieces = split_of(own)
    f32, bf16 = jnp.float32, jnp.bfloat16
    vmem = pl.BlockSpec(memory_space=pltpu.VMEM)
    hbm = pl.BlockSpec(memory_space=pl.ANY)
    dma = pltpu.SemaphoreType.DMA
    summed, sq, kept, w, mo, se = pl.pallas_call(
        functools.partial(exchange_kernel, n, reps, hot),
        out_shape=(
            pltpu.VMEM((own, packed), f32),
            pltpu.VMEM((blocks, LANES), f32),
            pltpu.VMEM(cold_sums.shape[1:], bf16),
            pltpu.VMEM(weight.shape, f32),
            pltpu.VMEM(weight.shape, f32),
            pltpu.VMEM(weight.shape, f32),
        ),
        in_specs=[pl.BlockSpec(memory_space=pltpu.HBM)] * 7,
        out_specs=(vmem,) * 6,
        scratch_shapes=[
            pltpu.SMEM(ranks.shape, ranks.dtype),
            pltpu.VMEM((chunks, tokens, chunk), bf16),
            pltpu.VMEM((tokens, width), bf16),
            pltpu.VMEM((tokens, width), bf16),
            pltpu.VMEM((chunks, chunk, width), bf16),
            pltpu.VMEM((n, cross_rows, packed), f32),
            pltpu.VMEM((m, 2 * line_rows, packed), f32),
            pltpu.VMEM((m, cross_rows, packed), f32),
            pltpu.VMEM((line_rows, packed), f32),
            pltpu.VMEM((m + 1, cross_rows, packed), f32),
            pltpu.VMEM((m + 1, 2 * line_rows, packed), f32),
            pltpu.VMEM((blocks, 8, LANES), f32),
            pltpu.VMEM((reps, blocks, LANES), f32),
            pltpu.VMEM((2, blocks, LANES), f32),
            pltpu.VMEM((m, blocks, LANES), f32),
            dma((2, chunks)),
            dma((5,)),
            dma,
            dma((m, pieces)),
            dma,
            dma((m + 1, pieces)),
            dma,
            dma((m + 1,)),
            dma,
            dma,
            dma,
            dma,
            dma,
            dma,
            dma,
            dma,
            pltpu.SemaphoreType.REGULAR,
            pltpu.SemaphoreType.REGULAR,
        ],
        compiler_params=pltpu.CompilerParams(
            collective_id=0, has_side_effects=True, vmem_limit_bytes=VMEM_GRANT
        ),
        name="exchange",
    )(ranks, features, out_grads, cold_sums, weight, moment, second)
    new_weight, new_moment, new_second, new_cold, column_sq = pl.pallas_call(
        functools.partial(update_kernel, n, rows * reps, tokens, hot),
        out_shape=(
            jax.ShapeDtypeStruct(weight.shape, f32),
            jax.ShapeDtypeStruct(weight.shape, f32),
            jax.ShapeDtypeStruct(weight.shape, f32),
            jax.ShapeDtypeStruct(cold_sums.shape, bf16),
            jax.ShapeDtypeStruct((blocks, LANES), f32),
        ),
        in_specs=[hbm] + [vmem] * 6,
        out_specs=(hbm,) * 5,
        scratch_shapes=[
            pltpu.SMEM(ranks.shape, ranks.dtype),
            pltpu.VMEM((3, weight.shape[0], packed), f32),
            pltpu.VMEM((blocks, LANES), f32),
            dma,
            dma((3, blocks)),
            dma,
            dma,
        ],
        compiler_params=pltpu.CompilerParams(vmem_limit_bytes=VMEM_GRANT // 2),
        name="update",
    )(ranks, summed, sq, kept, w, mo, se)
    return new_weight, new_moment, new_second, new_cold, column_sq.reshape(width)


def solution(mesh):
    owned = P(("rep", "dp"), None)
    placed = (P("dp", "rep"), P("dp", None), P("dp", "rep", None), owned, owned, owned, P())
    return jax.shard_map(
        functools.partial(body, mesh.shape["dp"], mesh.shape["rep"]),
        mesh=mesh,
        in_specs=placed,
        out_specs=(owned, owned, owned, P("dp", "rep", None), P()),
        check_vma=False,
    )
```

time: 54.3 us -> 50.6 us (0.932)
  Pallas kernels: 53.5 us -> 49.8 us
    pallas_call x1, Pallas kernels: 49.6 us -> 46.6 us  [body(): pl.pallas_call(functools.partial(exchange_kernel, n, reps, hot), out_shap...]
    pallas_call x1, Pallas kernels: 3.82 us -> 3.18 us  [body(): pl.pallas_call(functools.partial(update_kernel, n, rows * reps, tokens, h...]
where the time goes in v3:
time: 50.6 us; the launch traced here: 50.4 us
  Pallas kernels  49.8 us (98%)
  between operations  0.66 us (1%)
    pallas_call x1, Pallas kernels, body(): pl.pallas_call(functools.partial(exchange_kernel, n, reps, hot), out_shap...  46.6 us
    pallas_call x1, Pallas kernels, body(): pl.pallas_call(functools.partial(update_kernel, n, rows * reps, tokens, h...  3.18 us

profile of v3, /device:TPU:0, one launch (start us, length us, event | category | flops | bytes accessed | tf_op | source)
XLA Modules:
  0.0 50.4 jit_solution(12292002610807293541)
XLA Ops:
  0.6 0.0 copy-start
  0.6 46.6 %exchange.1 = (f32[256,512]{1,0:T(8,128)S(1)}, f32[8,128]{1,0:T(8,128)S(1)}, bf16[2048,1024]{1,0:T(8,128)(2,1)S(1)}, f32[256,1024]{1,0:T(8,128)S(1)}, f32[256,1024]{1,0:T(8,128)S(1)}, /*index=5*/f32[256,1024]{1,0:T(8,128)S(1)}) custom-call(s32[8]{0:T(128)} %ranks_any.1, bf16[640,2048]{1,0:T(8,128)(2,1)} %feat.1, bf16[640,1024]{1,0:T(8,128)(2,1)} %og.1, ...), custom_call_target="tpu_custom_call" | custom-call | tf_op jit(solution)/shard_map/exchange/pallas_call | solution.py:494
  47.2 0.0 copy-done
  47.2 3.2 %update.1 = (f32[256,1024]{1,0:T(8,128)}, f32[256,1024]{1,0:T(8,128)}, f32[256,1024]{1,0:T(8,128)}, bf16[1,2048,1024]{2,1,0:T(8,128)(2,1)}, f32[8,128]{1,0:T(8,128)}) custom-call(s32[8]{0:T(128)S(1)} %copy-done, f32[256,512]{1,0:T(8,128)S(1)} %get-tuple-element.16.summed, f32[8,128]{1,0:T(8,128)S(1)} %get-tuple-element.17.sq, ...), custom_call_target="tpu_custom_call" | custom-call | tf_op jit(solution)/shard_map/update/pallas_call | solution.py:546
Async XLA Ops:
  0.6 46.6 %copy-start = (s32[8]{0:T(128)S(1)}, s32[8]{0:T(128)}, u32[]{:S(2)}) copy-start(s32[8]{0:T(128)} %ranks_any.1) | copy-start | bytes 100

commit v4 on v3

--- a/solution.py
+++ b/solution.py
@@ -8,6 +8,7 @@
 
 LANES = 128
 GROUP = 32
+LAG = 2
 FRONT = 6
 VMEM_GRANT = 55 * 2**20
 MESH = pl.DeviceIdType.MESH
@@ -25,16 +26,26 @@
     for b in range(blocks):
         gap = ranks[b] - rank
         found = found + b * (1 - jnp.minimum(gap * gap, 1))
-    return pl.multiple_of(found * LANES, LANES)
-
-
-def exchange_kernel(
+    return found
+
+
+def exchange_kernel(n, reps, hot, *refs):
+    feat = refs[1]
+    chunks = feat.shape[1] // max(feat.shape[1] // n, LANES)
+    dma = pltpu.SemaphoreType.DMA
+    pl.run_scoped(
+        functools.partial(exchange_body, n, reps, hot, *refs), dma((2, chunks)), dma((5,))
+    )
+
+
+def exchange_body(
     n, reps, hot,
     ranks_hbm, feat, og, cold, weight, moment, second,
     summed, sq_out, kept, w_out, m_out, s_out,
-    ranks, feat_v, og_v, og_p, cold_v, pack_a, pack_b, rx_a, rx_b, zin_a, zin_b, sq, reps_sq, pair_sq, line_sq,
-    in_sem, state_sem, x_send, x_recv, za_send, za_recv, zb_send, zb_recv, b_send, b_recv,
+    ranks, feat_v, og_v, cold_v, pack_a, pack_b, rx_a, rx_b, zin_a, zin_b, sq, reps_sq, pair_sq, line_sq,
+    x_send, x_recv, za_send, za_recv, zb_send, zb_recv, b_send, b_recv,
     nr_send, nr_recv, nx_send, nx_recv, nz_send, nz_recv, from_left, from_right,
+    in_sem, state_sem,
 ):
     m = n // 2
     tokens = feat.shape[0]
@@ -120,16 +131,6 @@
 
     sq[...] = jnp.zeros_like(sq)
 
-    def ranked(load, lo, hi):
-        parts = [load(slice(b * LANES, (b + 1) * LANES)) for b in range(blocks)]
-        found = []
-        for r in range(lo, hi):
-            held = parts[0]
-            for b in range(1, blocks):
-                held = jnp.where(ranks[b] == r, parts[b], held)
-            found.append(held)
-        return found
-
     def cross(k, sub):
         d = dest(k)
         at = pl.ds(pl.multiple_of(sub * part, 8), part)
@@ -148,11 +149,12 @@
             device_id={"dp": me + 2 if right else me - 2}, device_id_type=MESH,
         )
 
-    def along_b(d, right):
+    def along_b(d, s, right):
         slot = d + 1 if right else d
-        return pltpu.make_async_remote_copy(
-            src_ref=pack_b.at[d], dst_ref=zin_b.at[slot],
-            send_sem=zb_send, recv_sem=zb_recv.at[slot],
+        at = pl.ds(pl.multiple_of(s * line_rows, 8), line_rows)
+        return pltpu.make_async_remote_copy(
+            src_ref=pack_b.at[d, at], dst_ref=zin_b.at[slot, at],
+            send_sem=zb_send, recv_sem=zb_recv.at[slot, s],
             device_id={"dp": me + 2 if right else me - 2}, device_id_type=MESH,
         )
 
@@ -193,94 +195,101 @@
             device_id={"dp": me + 2 if right else me - 2}, device_id_type=MESH,
         )
 
-    def raw_b(k):
-        d = dest(k)
-
+    def raw_b(d, s):
         @pl.when(jnp.logical_and(d > p, p == 0))
         def _():
-            along_b(d, True).start()
+            along_b(d, s, True).start()
 
         @pl.when(jnp.logical_and(d < p, p == m - 1))
         def _():
-            along_b(d, False).start()
-
-    def permute(lo, hi):
-        for g in range(0, tokens, GROUP):
-            at = slice(g, min(g + GROUP, tokens))
-            for r, held in enumerate(ranked(lambda cols: og_v[at, cols], lo, hi), lo):
-                og_p[at, r * LANES:(r + 1) * LANES] = held
-
-    def product(i, lo, hi, store):
+            along_b(d, s, False).start()
+
+    def cross_step(k, subs=range(pieces)):
+        d = dest(k)
+        for sub in subs:
+            at = slice(sub * part, (sub + 1) * part)
+            cross(k, sub).wait_recv()
+            pack_a[2 * d + x, at] += rx_a[d, at]
+
+            @pl.when(jnp.logical_and(d >= p, p > 0))
+            def _():
+                along_a(d, sub, True).wait_recv()
+                pack_a[2 * d + x, at] += zin_a[d + 1, at]
+
+            @pl.when(jnp.logical_and(d <= p, p < m - 1))
+            def _():
+                along_a(d, sub, False).wait_recv()
+                pack_a[2 * d + x, at] += zin_a[d, at]
+
+            @pl.when(d > p)
+            def _():
+                along_a(d, sub, True).start()
+
+            @pl.when(d < p)
+            def _():
+                along_a(d, sub, False).start()
+
+            @pl.when(d == p)
+            def _():
+                summed[at] = pack_a[2 * d + x, at]
+
+    def fill(i, first=0, last=chunk):
+        c = chunk_at(i)
         grad = lax.dot_general(
-            feat_v[i], og_p[:, lo * LANES:hi * LANES], (((0,), (0,)), ((), ())),
+            feat_v[i, :, first:last], og_v[...], (((0,), (0,)), ((), ())),
             preferred_element_type=jnp.float32,
         )
-        squares = [sq[r] for r in range(lo, hi)]
-        for g in range(0, chunk, GROUP):
-            at = slice(g, g + GROUP)
-            held = ranked(lambda cols: cold_v[i, at, cols], lo, hi)
+        squares = [sq[b] for b in range(blocks)]
+        for g in range(first, last, GROUP):
             values = []
-            for t in range(hi - lo):
-                value = grad[at, t * LANES:(t + 1) * LANES] + held[t].astype(jnp.float32)
+            for b in range(blocks):
+                cols = slice(b * LANES, (b + 1) * LANES)
+                value = grad[g - first:g - first + GROUP, cols]
+                value += cold_v[i, g:g + GROUP, cols].astype(jnp.float32)
                 for h in range(0, GROUP, 8):
-                    squares[t] += value[h:h + 8] * value[h:h + 8]
+                    squares[b] += value[h:h + 8] * value[h:h + 8]
                 values.append(value)
-            store(g, values)
-        for r in range(lo, hi):
-            sq[r] = squares[r - lo]
-
-    def hot_fill(i):
-        c = chunk_at(i)
-
-        def store(g, values):
-            for h in range(0, GROUP, 8):
-                owner = c * inner + (g + h) // own
-                row = (g + h) % own
-                for r in range(hot):
-                    cols = slice(r * LANES, (r + 1) * LANES)
+            at = pl.ds(pl.multiple_of(c * chunk + g, 16), GROUP)
+            for b in range(blocks):
+                kept[at, b * LANES:(b + 1) * LANES] = jnp.where(
+                    ranks[b] < hot, jnp.zeros_like(values[b]), values[b]).astype(jnp.bfloat16)
+            for r in range(hot):
+                cols = slice(r * LANES, (r + 1) * LANES)
+                held = values[0]
+                for b in range(1, blocks):
+                    held = jnp.where(ranks[b] == r, values[b], held)
+                for h in range(0, GROUP, 8):
+                    owner = c * inner + (g + h) // own
+                    row = (g + h) % own
                     if row < cross_rows:
-                        pack_a[owner, row:row + 8, cols] = values[r][h:h + 8]
+                        pack_a[owner, row:row + 8, cols] = held[h:h + 8]
                     else:
-                        at = pl.ds(pl.multiple_of((owner % 2) * line_rows + row - cross_rows, 8), 8)
-                        pack_b[owner // 2, at, cols] = values[r][h:h + 8]
-
-        product(i, 0, hot, store)
-
-    def hot_step(i):
+                        to = pl.ds(pl.multiple_of((owner % 2) * line_rows + row - cross_rows, 8), 8)
+                        pack_b[owner // 2, to, cols] = held[h:h + 8]
+        for b in range(blocks):
+            sq[b] = squares[b]
+
+    def step(i):
         feat_copy(i).wait()
         cold_copy(i).wait()
-        hot_fill(i)
+        fill(i)
         if chunk == own:
-            k = i // 2
-            for sub in range(pieces):
-                @pl.when(jnp.logical_and(i % 2 == 0, k * pieces + sub < FRONT))
-                def _():
-                    cross(k, sub).start()
-
-            @pl.when(i % 2 == 1)
-            def _():
-                raw_b(k)
-
-    def cold_step(i):
-        c = chunk_at(i)
-
-        def store(g, values):
-            at = pl.ds(pl.multiple_of(c * chunk + g, 16), GROUP)
-            values = [value.astype(jnp.bfloat16) for value in values]
-            for b in range(blocks):
-                new = jnp.zeros_like(values[0])
-                for r in range(hot, blocks):
-                    new = jnp.where(ranks[b] == r, values[r - hot], new)
-                kept[at, b * LANES:(b + 1) * LANES] = new
-
-        product(i, hot, blocks, store)
+            send_cross(i)
+            raw_b(dest(i // 2), chunk_at(i) % 2)
+
+    def send_cross(i):
+        k = (i - lag) // 2
+        for sub in range(pieces):
+            @pl.when((i >= lag) & ((i - lag) % 2 == 0) & (k * pieces + sub < FRONT))
+            def _():
+                cross(k, sub).start()
 
     state[4].wait()
+    state[3].wait()
     feat_copy(0).wait()
     cold_copy(0).wait()
-    state[3].wait()
-    permute(0, hot)
-    hot_fill(0)
+    early = LANES if chunk == own else chunk
+    fill(0, 0, early)
     greeted = (p + m - 1) // m + (2 * m - 2 - p) // m + 1 + (reps - 1)
     pl.semaphore_wait(barrier, greeted)
 
@@ -292,21 +301,33 @@
     def _():
         token(False)
 
+    lag = rep % 2 * LAG
     if chunk == own:
-        for sub in range(min(pieces, FRONT)):
-            cross(0, sub).start()
-    rolled(1, chunks, hot_step)
+        ready = [sub for sub in range(pieces) if (sub + 1) * part <= early]
+        rest_of = [sub for sub in range(pieces) if (sub + 1) * part > early]
+
+        def start_early(subs):
+            @pl.when(lag == 0)
+            def _():
+                for sub in subs:
+                    cross(0, sub).start()
+
+        start_early(ready)
+        if early < chunk:
+            fill(0, early, chunk)
+        start_early(rest_of)
+        raw_b(dest(0), 1 - x)
+    rolled(1, chunks, step)
     for copy in state[:3]:
         copy.start()
-    permute(hot, blocks)
-    rolled(0, chunks, cold_step)
     if chunk != own:
         def launch(k):
             for sub in range(pieces):
                 @pl.when(k * pieces + sub < FRONT)
                 def _():
                     cross(k, sub).start()
-            raw_b(k)
+            for s in range(2):
+                raw_b(dest(k), s)
 
         rolled(0, m, launch)
     for r in range(blocks):
@@ -315,59 +336,32 @@
 
     def line_step(k):
         d = dest(k)
-
-        @pl.when(jnp.logical_and(d >= p, p > 0))
-        def _():
-            along_b(d, True).wait_recv()
-            pack_b[d] += zin_b[d + 1]
-
-        @pl.when(jnp.logical_and(d <= p, p < m - 1))
-        def _():
-            along_b(d, False).wait_recv()
-            pack_b[d] += zin_b[d]
-
-        @pl.when(jnp.logical_and(d > p, p > 0))
-        def _():
-            along_b(d, True).start()
-
-        @pl.when(jnp.logical_and(d < p, p < m - 1))
-        def _():
-            along_b(d, False).start()
+        for s in range(2):
+            at = slice(s * line_rows, (s + 1) * line_rows)
+
+            @pl.when(jnp.logical_and(d >= p, p > 0))
+            def _():
+                along_b(d, s, True).wait_recv()
+                pack_b[d, at] += zin_b[d + 1, at]
+
+            @pl.when(jnp.logical_and(d <= p, p < m - 1))
+            def _():
+                along_b(d, s, False).wait_recv()
+                pack_b[d, at] += zin_b[d, at]
+
+            @pl.when(jnp.logical_and(d > p, p > 0))
+            def _():
+                along_b(d, s, True).start()
+
+            @pl.when(jnp.logical_and(d < p, p < m - 1))
+            def _():
+                along_b(d, s, False).start()
 
     def rest(k):
         for sub in range(pieces):
             @pl.when(k * pieces + sub >= FRONT)
             def _():
                 cross(k, sub).start()
-
-    def cross_step(k, subs=range(pieces)):
-        d = dest(k)
-        for sub in subs:
-            at = slice(sub * part, (sub + 1) * part)
-            cross(k, sub).wait_recv()
-            pack_a[2 * d + x, at] += rx_a[d, at]
-
-            @pl.when(jnp.logical_and(d >= p, p > 0))
-            def _():
-                along_a(d, sub, True).wait_recv()
-                pack_a[2 * d + x, at] += zin_a[d + 1, at]
-
-            @pl.when(jnp.logical_and(d <= p, p < m - 1))
-            def _():
-                along_a(d, sub, False).wait_recv()
-                pack_a[2 * d + x, at] += zin_a[d, at]
-
-            @pl.when(d > p)
-            def _():
-                along_a(d, sub, True).start()
-
-            @pl.when(d < p)
-            def _():
-                along_a(d, sub, False).start()
-
-            @pl.when(d == p)
-            def _():
-                summed[at] = pack_a[2 * d + x, at]
 
     span(0, m - 1, line_step)
 
@@ -424,7 +418,7 @@
     bytes_of(rx_a, x_send, x_recv.at[0, 0]).wait_send()
     if m > 1:
         bytes_of(zin_a.at[pl.ds(0, m - 1)], za_send, za_recv.at[0, 0]).wait_send()
-        bytes_of(zin_b.at[pl.ds(0, m - 1)], zb_send, zb_recv.at[0]).wait_send()
+        bytes_of(zin_b.at[pl.ds(0, m - 1)], zb_send, zb_recv.at[0, 0]).wait_send()
         bytes_of(line_sq.at[pl.ds(0, m - 1)], nz_send, nz_recv).wait_send()
     cross_b().wait_send()
     norm_x().wait_send()
@@ -435,7 +429,7 @@
     n, total_rows, tokens, hot,
     ranks_any, summed, sq, kept, weight, moment, second,
     w_hbm, m_hbm, s_hbm, nc_hbm, sq_hbm,
-    ranks, fresh, sq_v, nc_sem, state_sem, sq_sem, ranks_sem,
+    ranks, fresh, nc_sem, state_sem, sq_sem, ranks_sem,
 ):
     width = weight.shape[1]
     blocks = width // LANES
@@ -449,17 +443,16 @@
     order = pltpu.make_async_copy(ranks_any, ranks, ranks_sem)
     order.start()
     send(kept, nc_hbm.at[0], nc_sem)
+    send(sq, sq_hbm, sq_sem)
     order.wait()
-    where = [pl.ds(block_of(ranks, blocks, r), LANES) for r in range(blocks)]
+    block = [block_of(ranks, blocks, r) for r in range(blocks)]
+    where = [pl.ds(pl.multiple_of(b * LANES, LANES), LANES) for b in block]
     for r in range(hot, blocks):
         for i, src in enumerate((weight, moment, second)):
             send(src.at[:, where[r]], outs[i].at[:, where[r]], state_sem.at[i, r])
-    for b in range(blocks):
-        sq_v[b:b + 1, :] = sq[pl.ds(ranks[b], 1), :]
-    send(sq_v, sq_hbm, sq_sem)
     for r in range(hot):
         cols = slice(r * LANES, (r + 1) * LANES)
-        rms = jnp.sqrt(sq[r:r + 1, :] / jnp.float32(total_rows * n * tokens))
+        rms = jnp.sqrt(sq[pl.ds(block[r], 1), :] / jnp.float32(total_rows * n * tokens))
         clip = 1.0 / jnp.maximum(jnp.float32(1.0), rms)
         grad = summed[:, cols] * clip / jnp.float32(n)
         moved = 0.9 * moment[:, where[r]] + 0.1 * grad
@@ -507,7 +500,6 @@
             pltpu.SMEM(ranks.shape, ranks.dtype),
             pltpu.VMEM((chunks, tokens, chunk), bf16),
             pltpu.VMEM((tokens, width), bf16),
-            pltpu.VMEM((tokens, width), bf16),
             pltpu.VMEM((chunks, chunk, width), bf16),
             pltpu.VMEM((n, cross_rows, packed), f32),
             pltpu.VMEM((m, 2 * line_rows, packed), f32),
@@ -519,14 +511,12 @@
             pltpu.VMEM((reps, blocks, LANES), f32),
             pltpu.VMEM((2, blocks, LANES), f32),
             pltpu.VMEM((m, blocks, LANES), f32),
-            dma((2, chunks)),
-            dma((5,)),
             dma,
             dma((m, pieces)),
             dma,
             dma((m + 1, pieces)),
             dma,
-            dma((m + 1,)),
+            dma((m + 1, 2)),
             dma,
             dma,
             dma,
@@ -557,7 +547,6 @@
         scratch_shapes=[
             pltpu.SMEM(ranks.shape, ranks.dtype),
             pltpu.VMEM((3, weight.shape[0], packed), f32),
-            pltpu.VMEM((blocks, LANES), f32),
             dma,
             dma((3, blocks)),
             dma,

time: 50.6 us -> 50.1 us (level); the launches traced: 50.4 us -> 49.2 us
  Pallas kernels: 49.8 us -> 48.6 us
    pallas_call x1, Pallas kernels: 46.6 us -> 45.4 us  [body(): pl.pallas_call(functools.partial(exchange_kernel, n, reps, hot), out_shap...]
where the time goes in v4:
time: 50.1 us; the launch traced here: 49.2 us
  Pallas kernels  48.6 us (97%)
  between operations  0.66 us (1%)
    pallas_call x1, Pallas kernels, body(): pl.pallas_call(functools.partial(exchange_kernel, n, reps, hot), out_shap...  45.4 us
    pallas_call x1, Pallas kernels, body(): pl.pallas_call(functools.partial(update_kernel, n, rows * reps, tokens, h...  3.18 us

profile of v4, /device:TPU:0, one launch (start us, length us, event | category | flops | bytes accessed | tf_op | source)
XLA Modules:
  0.0 49.2 jit_solution(3206622595136349745)
XLA Ops:
  0.6 0.0 copy-start
  0.6 45.4 %exchange.1 = (f32[256,512]{1,0:T(8,128)S(1)}, f32[8,128]{1,0:T(8,128)S(1)}, bf16[2048,1024]{1,0:T(8,128)(2,1)S(1)}, f32[256,1024]{1,0:T(8,128)S(1)}, f32[256,1024]{1,0:T(8,128)S(1)}, /*index=5*/f32[256,1024]{1,0:T(8,128)S(1)}) custom-call(s32[8]{0:T(128)} %ranks_any.1, bf16[640,2048]{1,0:T(8,128)(2,1)} %refs_1_.1, bf16[640,1024]{1,0:T(8,128)(2,1)} %refs_2_.1, ...), custom_call_target="tpu_custom_call" | custom-call | tf_op jit(solution)/shard_map/exchange/pallas_call | solution.py:487
  46.0 0.0 copy-done
  46.0 3.2 %update.1 = (f32[256,1024]{1,0:T(8,128)}, f32[256,1024]{1,0:T(8,128)}, f32[256,1024]{1,0:T(8,128)}, bf16[1,2048,1024]{2,1,0:T(8,128)(2,1)}, f32[8,128]{1,0:T(8,128)}) custom-call(s32[8]{0:T(128)S(1)} %copy-done, f32[256,512]{1,0:T(8,128)S(1)} %get-tuple-element.16.summed, f32[8,128]{1,0:T(8,128)S(1)} %get-tuple-element.17.sq, ...), custom_call_target="tpu_custom_call" | custom-call | tf_op jit(solution)/shard_map/update/pallas_call | solution.py:536
Async XLA Ops:
  0.6 45.4 %copy-start = (s32[8]{0:T(128)S(1)}, s32[8]{0:T(128)}, u32[]{:S(2)}) copy-start(s32[8]{0:T(128)} %ranks_any.1) | copy-start | bytes 100

commit v5 on v4

--- a/solution.py
+++ b/solution.py
@@ -8,6 +8,7 @@
 
 LANES = 128
 GROUP = 32
+EXTRA = 86
 LAG = 2
 FRONT = 6
 VMEM_GRANT = 55 * 2**20
@@ -17,8 +18,9 @@
 def split_of(own):
     line = 8 * max(round(own / 48), 1)
     cross = own - line
-    pieces = next(s for s in (3, 2, 1) if cross % (8 * s) == 0)
-    return cross, line, pieces
+    extra = 8 * max(round(own / EXTRA), 1)
+    head = 8 * ((cross - extra + 8) // 16)
+    return cross, line, ((0, head), (head, cross - extra - head), (cross - extra, extra))
 
 
 def block_of(ranks, blocks, rank):
@@ -42,8 +44,8 @@
     n, reps, hot,
     ranks_hbm, feat, og, cold, weight, moment, second,
     summed, sq_out, kept, w_out, m_out, s_out,
-    ranks, feat_v, og_v, cold_v, pack_a, pack_b, rx_a, rx_b, zin_a, zin_b, sq, reps_sq, pair_sq, line_sq,
-    x_send, x_recv, za_send, za_recv, zb_send, zb_recv, b_send, b_recv,
+    ranks, feat_v, og_v, cold_v, pack_a, pack_b, rx_a, rx_b, rx_e, zin_a, zin_b, zin_e, sq, reps_sq, pair_sq, line_sq,
+    x_send, xe_send, x_recv, zx_send, ze_send, ze_recv, be_send, be_recv, za_send, za_recv, zb_send, zb_recv, b_send, b_recv,
     nr_send, nr_recv, nx_send, nx_recv, nz_send, nz_recv, from_left, from_right,
     in_sem, state_sem,
 ):
@@ -57,7 +59,9 @@
     chunks = rows // chunk
     inner = chunk // own
     cross_rows, line_rows, pieces = split_of(own)
-    part = cross_rows // pieces
+    subs_all = range(len(pieces))
+    kept_rows, extra_rows = pieces[-1]
+    extra = slice(kept_rows, cross_rows)
     me = lax.axis_index("dp")
     rep = lax.axis_index("rep")
     x = me % 2
@@ -133,20 +137,42 @@
 
     def cross(k, sub):
         d = dest(k)
-        at = pl.ds(pl.multiple_of(sub * part, 8), part)
+        at = pl.ds(*pieces[sub])
         return pltpu.make_async_remote_copy(
             src_ref=pack_a.at[2 * d + 1 - x, at], dst_ref=rx_a.at[d, at],
-            send_sem=x_send, recv_sem=x_recv.at[d, sub],
+            send_sem=xe_send if sub == subs_all[-1] else x_send, recv_sem=x_recv.at[d, sub],
             device_id={"dp": partner}, device_id_type=MESH,
         )
 
+    def start_cross(k, sub):
+        if sub == subs_all[-1]:
+            @pl.when(dest(k) != m - 1)
+            def _():
+                cross(k, sub).start()
+        else:
+            cross(k, sub).start()
+
     def along_a(d, sub, right):
-        at = pl.ds(pl.multiple_of(sub * part, 8), part)
+        at = pl.ds(*pieces[sub])
         slot = d + 1 if right else d
         return pltpu.make_async_remote_copy(
             src_ref=pack_a.at[2 * d + x, at], dst_ref=zin_a.at[slot, at],
-            send_sem=za_send, recv_sem=za_recv.at[slot, sub],
+            send_sem=zx_send if sub == subs_all[-1] else za_send, recv_sem=za_recv.at[slot, sub],
             device_id={"dp": me + 2 if right else me - 2}, device_id_type=MESH,
+        )
+
+    def along_e(s):
+        return pltpu.make_async_remote_copy(
+            src_ref=pack_a.at[2 * (m - 1) + s, pl.ds(kept_rows, extra_rows)], dst_ref=zin_e.at[s],
+            send_sem=ze_send, recv_sem=ze_recv.at[s],
+            device_id={"dp": me + 2}, device_id_type=MESH,
+        )
+
+    def cross_e():
+        return pltpu.make_async_remote_copy(
+            src_ref=pack_a.at[2 * (m - 1) + 1 - x, pl.ds(kept_rows, extra_rows)], dst_ref=rx_e,
+            send_sem=be_send, recv_sem=be_recv,
+            device_id={"dp": partner}, device_id_type=MESH,
         )
 
     def along_b(d, s, right):
@@ -200,38 +226,50 @@
         def _():
             along_b(d, s, True).start()
 
+        @pl.when((d == m - 1) & (d > p) & (p == 0))
+        def _():
+            along_e(s).start()
+
         @pl.when(jnp.logical_and(d < p, p == m - 1))
         def _():
             along_b(d, s, False).start()
 
-    def cross_step(k, subs=range(pieces)):
+    def cross_step(k, subs=subs_all):
         d = dest(k)
         for sub in subs:
-            at = slice(sub * part, (sub + 1) * part)
-            cross(k, sub).wait_recv()
-            pack_a[2 * d + x, at] += rx_a[d, at]
-
-            @pl.when(jnp.logical_and(d >= p, p > 0))
-            def _():
-                along_a(d, sub, True).wait_recv()
-                pack_a[2 * d + x, at] += zin_a[d + 1, at]
-
-            @pl.when(jnp.logical_and(d <= p, p < m - 1))
-            def _():
-                along_a(d, sub, False).wait_recv()
-                pack_a[2 * d + x, at] += zin_a[d, at]
-
-            @pl.when(d > p)
-            def _():
-                along_a(d, sub, True).start()
-
-            @pl.when(d < p)
-            def _():
-                along_a(d, sub, False).start()
-
-            @pl.when(d == p)
-            def _():
-                summed[at] = pack_a[2 * d + x, at]
+            if sub == subs_all[-1]:
+                @pl.when(d != m - 1)
+                def _():
+                    cross_piece(k, d, sub)
+            else:
+                cross_piece(k, d, sub)
+
+    def cross_piece(k, d, sub):
+        at = slice(pieces[sub][0], sum(pieces[sub]))
+        cross(k, sub).wait_recv()
+        pack_a[2 * d + x, at] += rx_a[d, at]
+
+        @pl.when(jnp.logical_and(d >= p, p > 0))
+        def _():
+            along_a(d, sub, True).wait_recv()
+            pack_a[2 * d + x, at] += zin_a[d + 1, at]
+
+        @pl.when(jnp.logical_and(d <= p, p < m - 1))
+        def _():
+            along_a(d, sub, False).wait_recv()
+            pack_a[2 * d + x, at] += zin_a[d, at]
+
+        @pl.when(d > p)
+        def _():
+            along_a(d, sub, True).start()
+
+        @pl.when(d < p)
+        def _():
+            along_a(d, sub, False).start()
+
+        @pl.when(d == p)
+        def _():
+            summed[at] = pack_a[2 * d + x, at]
 
     def fill(i, first=0, last=chunk):
         c = chunk_at(i)
@@ -279,10 +317,10 @@
 
     def send_cross(i):
         k = (i - lag) // 2
-        for sub in range(pieces):
-            @pl.when((i >= lag) & ((i - lag) % 2 == 0) & (k * pieces + sub < FRONT))
-            def _():
-                cross(k, sub).start()
+        for sub in subs_all:
+            @pl.when((i >= lag) & ((i - lag) % 2 == 0) & (k * len(pieces) + sub < FRONT))
+            def _():
+                start_cross(k, sub)
 
     state[4].wait()
     state[3].wait()
@@ -303,14 +341,14 @@
 
     lag = rep % 2 * LAG
     if chunk == own:
-        ready = [sub for sub in range(pieces) if (sub + 1) * part <= early]
-        rest_of = [sub for sub in range(pieces) if (sub + 1) * part > early]
+        ready = [sub for sub in subs_all if sum(pieces[sub]) <= early]
+        rest_of = [sub for sub in subs_all if sum(pieces[sub]) > early]
 
         def start_early(subs):
             @pl.when(lag == 0)
             def _():
                 for sub in subs:
-                    cross(0, sub).start()
+                    start_cross(0, sub)
 
         start_early(ready)
         if early < chunk:
@@ -322,10 +360,10 @@
         copy.start()
     if chunk != own:
         def launch(k):
-            for sub in range(pieces):
-                @pl.when(k * pieces + sub < FRONT)
+            for sub in subs_all:
+                @pl.when(k * len(pieces) + sub < FRONT)
                 def _():
-                    cross(k, sub).start()
+                    start_cross(k, sub)
             for s in range(2):
                 raw_b(dest(k), s)
 
@@ -357,11 +395,20 @@
             def _():
                 along_b(d, s, False).start()
 
+            @pl.when((d == m - 1) & (p > 0))
+            def _():
+                along_e(s).wait_recv()
+                pack_a[2 * d + s, extra] += zin_e[s]
+
+            @pl.when((d == m - 1) & (p > 0) & (p < m - 1))
+            def _():
+                along_e(s).start()
+
     def rest(k):
-        for sub in range(pieces):
-            @pl.when(k * pieces + sub >= FRONT)
-            def _():
-                cross(k, sub).start()
+        for sub in subs_all:
+            @pl.when(k * len(pieces) + sub >= FRONT)
+            def _():
+                start_cross(k, sub)
 
     span(0, m - 1, line_step)
 
@@ -382,7 +429,7 @@
     norm_x().start()
     rolled(0, m, rest)
     if m > 1:
-        cross_step(0, range(1, pieces))
+        cross_step(0, subs_all[1:])
     if m > 2:
         cross_step(1)
     norm_x().wait_recv()
@@ -400,6 +447,11 @@
     span(2, m - 2, cross_step)
     line_step(m - 1)
     cross_b().start()
+
+    @pl.when(p == m - 1)
+    def _():
+        cross_e().start()
+
     if m > 3:
         cross_step(m - 2)
     if m > 1:
@@ -415,11 +467,31 @@
     mine = pl.ds(pl.multiple_of(x * line_rows, 8), line_rows)
     summed[cross_rows:] = pack_b[p, mine] + rx_b[...]
 
-    bytes_of(rx_a, x_send, x_recv.at[0, 0]).wait_send()
+    @pl.when(p == m - 1)
+    def _():
+        cross_e().wait_recv()
+        summed[extra] = pack_a[2 * p + x, extra] + rx_e[...]
+        cross_e().wait_send()
+
+
+    main, tail = pl.ds(0, kept_rows), pl.ds(kept_rows, extra_rows)
+    bytes_of(rx_a.at[:, main], x_send, x_recv.at[0, 0]).wait_send()
     if m > 1:
-        bytes_of(zin_a.at[pl.ds(0, m - 1)], za_send, za_recv.at[0, 0]).wait_send()
+        bytes_of(rx_a.at[pl.ds(0, m - 1), tail], xe_send, x_recv.at[0, 0]).wait_send()
+        bytes_of(zin_a.at[pl.ds(0, m - 1), main], za_send, za_recv.at[0, 0]).wait_send()
         bytes_of(zin_b.at[pl.ds(0, m - 1)], zb_send, zb_recv.at[0, 0]).wait_send()
         bytes_of(line_sq.at[pl.ds(0, m - 1)], nz_send, nz_recv).wait_send()
+
+        @pl.when(p == m - 1)
+        def _():
+            bytes_of(zin_a.at[pl.ds(0, m - 1), tail], zx_send, za_recv.at[0, 0]).wait_send()
+
+        @pl.when(p < m - 1)
+        def _():
+            if m > 2:
+                bytes_of(zin_a.at[pl.ds(0, m - 2), tail], zx_send, za_recv.at[0, 0]).wait_send()
+            bytes_of(zin_e, ze_send, ze_recv.at[0]).wait_send()
+
     cross_b().wait_send()
     norm_x().wait_send()
     bytes_of(reps_sq.at[pl.ds(0, reps - 1)], nr_send, nr_recv).wait_send()
@@ -480,6 +552,8 @@
     chunk = max(own, LANES)
     chunks = rows // chunk
     cross_rows, line_rows, pieces = split_of(own)
+    extra_rows = pieces[-1][1]
+    pieces = len(pieces)
     f32, bf16 = jnp.float32, jnp.bfloat16
     vmem = pl.BlockSpec(memory_space=pltpu.VMEM)
     hbm = pl.BlockSpec(memory_space=pl.ANY)
@@ -505,14 +579,22 @@
             pltpu.VMEM((m, 2 * line_rows, packed), f32),
             pltpu.VMEM((m, cross_rows, packed), f32),
             pltpu.VMEM((line_rows, packed), f32),
+            pltpu.VMEM((extra_rows, packed), f32),
             pltpu.VMEM((m + 1, cross_rows, packed), f32),
             pltpu.VMEM((m + 1, 2 * line_rows, packed), f32),
+            pltpu.VMEM((2, extra_rows, packed), f32),
             pltpu.VMEM((blocks, 8, LANES), f32),
             pltpu.VMEM((reps, blocks, LANES), f32),
             pltpu.VMEM((2, blocks, LANES), f32),
             pltpu.VMEM((m, blocks, LANES), f32),
             dma,
+            dma,
             dma((m, pieces)),
+            dma,
+            dma,
+            dma((2,)),
+            dma,
+            dma,
             dma,
             dma((m + 1, pieces)),
             dma,

time: 50.1 us -> 49.4 us (0.986)
  no operation moved by 1% of the time
where the time goes in v5:
time: 49.4 us; the launch traced here: 48.8 us
  Pallas kernels  48.1 us (97%)
  between operations  0.66 us (1%)
    pallas_call x1, Pallas kernels, body(): pl.pallas_call(functools.partial(exchange_kernel, n, reps, hot), out_shap...  44.9 us
    pallas_call x1, Pallas kernels, body(): pl.pallas_call(functools.partial(update_kernel, n, rows * reps, tokens, h...  3.18 us

profile of v5, /device:TPU:0, one launch (start us, length us, event | category | flops | bytes accessed | tf_op | source)
XLA Modules:
  0.0 48.8 jit_solution(3013955026555296636)
XLA Ops:
  0.6 0.0 copy-start
  0.6 44.9 %exchange.1 = (f32[256,512]{1,0:T(8,128)S(1)}, f32[8,128]{1,0:T(8,128)S(1)}, bf16[2048,1024]{1,0:T(8,128)(2,1)S(1)}, f32[256,1024]{1,0:T(8,128)S(1)}, f32[256,1024]{1,0:T(8,128)S(1)}, /*index=5*/f32[256,1024]{1,0:T(8,128)S(1)}) custom-call(s32[8]{0:T(128)} %ranks_any.1, bf16[640,2048]{1,0:T(8,128)(2,1)} %refs_1_.1, bf16[640,1024]{1,0:T(8,128)(2,1)} %refs_2_.1, ...), custom_call_target="tpu_custom_call" | custom-call | tf_op jit(solution)/shard_map/exchange/pallas_call | solution.py:561
  45.6 0.0 copy-done
  45.6 3.2 %update.1 = (f32[256,1024]{1,0:T(8,128)}, f32[256,1024]{1,0:T(8,128)}, f32[256,1024]{1,0:T(8,128)}, bf16[1,2048,1024]{2,1,0:T(8,128)(2,1)}, f32[8,128]{1,0:T(8,128)}) custom-call(s32[8]{0:T(128)S(1)} %copy-done, f32[256,512]{1,0:T(8,128)S(1)} %get-tuple-element.16.summed, f32[8,128]{1,0:T(8,128)S(1)} %get-tuple-element.17.sq, ...), custom_call_target="tpu_custom_call" | custom-call | tf_op jit(solution)/shard_map/update/pallas_call | solution.py:618
Async XLA Ops:
  0.6 44.9 %copy-start = (s32[8]{0:T(128)S(1)}, s32[8]{0:T(128)}, u32[]{:S(2)}) copy-start(s32[8]{0:T(128)} %ranks_any.1) | copy-start | bytes 100

commit v6 on v5

--- a/solution.py
+++ b/solution.py
@@ -32,11 +32,39 @@
 
 
 def exchange_kernel(n, reps, hot, *refs):
-    feat = refs[1]
-    chunks = feat.shape[1] // max(feat.shape[1] // n, LANES)
+    rows = refs[1].shape[1]
+    own = rows // n
+    chunks = rows // max(own, LANES)
+    m = n // 2
+    pieces = len(split_of(own)[2])
     dma = pltpu.SemaphoreType.DMA
+    regular = pltpu.SemaphoreType.REGULAR
     pl.run_scoped(
-        functools.partial(exchange_body, n, reps, hot, *refs), dma((2, chunks)), dma((5,))
+        functools.partial(exchange_body, n, reps, hot, *refs),
+        dma,
+        dma,
+        dma((m, pieces)),
+        dma,
+        dma,
+        dma((2,)),
+        dma,
+        dma,
+        dma,
+        dma((m + 1, pieces)),
+        dma,
+        dma((m + 1, 2)),
+        dma,
+        dma,
+        dma,
+        dma,
+        dma,
+        dma,
+        dma,
+        dma,
+        regular,
+        regular,
+        dma((2, chunks)),
+        dma((5,)),
     )
 
 
@@ -497,7 +525,16 @@
     bytes_of(reps_sq.at[pl.ds(0, reps - 1)], nr_send, nr_recv).wait_send()
 
 
-def update_kernel(
+def update_kernel(n, total_rows, tokens, hot, *refs):
+    blocks = refs[4].shape[1] // LANES
+    dma = pltpu.SemaphoreType.DMA
+    pl.run_scoped(
+        functools.partial(update_body, n, total_rows, tokens, hot, *refs),
+        dma, dma((3, blocks)), dma, dma,
+    )
+
+
+def update_body(
     n, total_rows, tokens, hot,
     ranks_any, summed, sq, kept, weight, moment, second,
     w_hbm, m_hbm, s_hbm, nc_hbm, sq_hbm,
@@ -553,11 +590,9 @@
     chunks = rows // chunk
     cross_rows, line_rows, pieces = split_of(own)
     extra_rows = pieces[-1][1]
-    pieces = len(pieces)
     f32, bf16 = jnp.float32, jnp.bfloat16
     vmem = pl.BlockSpec(memory_space=pltpu.VMEM)
     hbm = pl.BlockSpec(memory_space=pl.ANY)
-    dma = pltpu.SemaphoreType.DMA
     summed, sq, kept, w, mo, se = pl.pallas_call(
         functools.partial(exchange_kernel, n, reps, hot),
         out_shape=(
@@ -587,28 +622,6 @@
             pltpu.VMEM((reps, blocks, LANES), f32),
             pltpu.VMEM((2, blocks, LANES), f32),
             pltpu.VMEM((m, blocks, LANES), f32),
-            dma,
-            dma,
-            dma((m, pieces)),
-            dma,
-            dma,
-            dma((2,)),
-            dma,
-            dma,
-            dma,
-            dma((m + 1, pieces)),
-            dma,
-            dma((m + 1, 2)),
-            dma,
-            dma,
-            dma,
-            dma,
-            dma,
-            dma,
-            dma,
-            dma,
-            pltpu.SemaphoreType.REGULAR,
-            pltpu.SemaphoreType.REGULAR,
         ],
         compiler_params=pltpu.CompilerParams(
             collective_id=0, has_side_effects=True, vmem_limit_bytes=VMEM_GRANT
@@ -629,10 +642,6 @@
         scratch_shapes=[
             pltpu.SMEM(ranks.shape, ranks.dtype),
             pltpu.VMEM((3, weight.shape[0], packed), f32),
-            dma,
-            dma((3, blocks)),
-            dma,
-            dma,
         ],
         compiler_params=pltpu.CompilerParams(vmem_limit_bytes=VMEM_GRANT // 2),
         name="update",

time: 49.4 us -> 48.6 us (0.984)
  Pallas kernels: 48.1 us -> 47.3 us
    pallas_call x1, Pallas kernels: 44.9 us -> 44.4 us  [body(): pl.pallas_call(functools.partial(exchange_kernel, n, reps, hot), out_shap...]
where the time goes in v6:
time: 48.6 us; the launch traced here: 48 us
  Pallas kernels  47.3 us (97%)
  between operations  0.64 us (1%)
    pallas_call x1, Pallas kernels, body(): pl.pallas_call(functools.partial(exchange_kernel, n, reps, hot), out_shap...  44.4 us
    pallas_call x1, Pallas kernels, body(): pl.pallas_call(functools.partial(update_kernel, n, rows * reps, tokens, h...  2.94 us

profile of v6, /device:TPU:0, one launch (start us, length us, event | category | flops | bytes accessed | tf_op | source)
XLA Modules:
  0.0 48.0 jit_solution(14984781468171836258)
XLA Ops:
  0.6 0.0 copy-start
  0.6 44.4 %exchange.1 = (f32[256,512]{1,0:T(8,128)S(1)}, f32[8,128]{1,0:T(8,128)S(1)}, bf16[2048,1024]{1,0:T(8,128)(2,1)S(1)}, f32[256,1024]{1,0:T(8,128)S(1)}, f32[256,1024]{1,0:T(8,128)S(1)}, /*index=5*/f32[256,1024]{1,0:T(8,128)S(1)}) custom-call(s32[8]{0:T(128)} %refs_0_.3, bf16[640,2048]{1,0:T(8,128)(2,1)} %refs_1_.1, bf16[640,1024]{1,0:T(8,128)(2,1)} %refs_2_.1, ...), custom_call_target="tpu_custom_call" | custom-call | tf_op jit(solution)/shard_map/exchange/pallas_call | solution.py:596
  45.0 0.0 copy-done
  45.1 2.9 %update.1 = (f32[256,1024]{1,0:T(8,128)}, f32[256,1024]{1,0:T(8,128)}, f32[256,1024]{1,0:T(8,128)}, bf16[1,2048,1024]{2,1,0:T(8,128)(2,1)}, f32[8,128]{1,0:T(8,128)}) custom-call(s32[8]{0:T(128)S(1)} %copy-done, f32[256,512]{1,0:T(8,128)S(1)} %get-tuple-element.16.refs_1_, f32[8,128]{1,0:T(8,128)S(1)} %get-tuple-element.17.refs_2_, ...), custom_call_target="tpu_custom_call" | custom-call | tf_op jit(solution)/shard_map/update/pallas_call | solution.py:631
Async XLA Ops:
  0.6 44.4 %copy-start = (s32[8]{0:T(128)S(1)}, s32[8]{0:T(128)}, u32[]{:S(2)}) copy-start(s32[8]{0:T(128)} %refs_0_.3) | copy-start | bytes 100

commit v7 on v6

--- a/solution.py
+++ b/solution.py
@@ -9,7 +9,7 @@
 LANES = 128
 GROUP = 32
 EXTRA = 86
-LAG = 2
+LAG = 1
 FRONT = 6
 VMEM_GRANT = 55 * 2**20
 MESH = pl.DeviceIdType.MESH
@@ -65,6 +65,7 @@
         regular,
         dma((2, chunks)),
         dma((5,)),
+        dma((2, 2)),
     )
 
 
@@ -75,7 +76,7 @@
     ranks, feat_v, og_v, cold_v, pack_a, pack_b, rx_a, rx_b, rx_e, zin_a, zin_b, zin_e, sq, reps_sq, pair_sq, line_sq,
     x_send, xe_send, x_recv, zx_send, ze_send, ze_recv, be_send, be_recv, za_send, za_recv, zb_send, zb_recv, b_send, b_recv,
     nr_send, nr_recv, nx_send, nx_recv, nz_send, nz_recv, from_left, from_right,
-    in_sem, state_sem,
+    in_sem, state_sem, first_sem,
 ):
     m = n // 2
     tokens = feat.shape[0]
@@ -144,9 +145,26 @@
         feat_copy(i).start()
         cold_copy(i).start()
 
+    early = LANES if chunk == own else chunk
+    start = chunk_at(0) * chunk
+
+    def first_feat(lo, hi):
+        cols = pl.ds(pl.multiple_of(start + lo, LANES), hi - lo)
+        return pltpu.make_async_copy(
+            feat.at[:, cols], feat_v.at[0, :, pl.ds(lo, hi - lo)], first_sem.at[0, lo // early])
+
+    def first_cold(lo, hi):
+        at = pl.ds(pl.multiple_of(start + lo, LANES), hi - lo)
+        return pltpu.make_async_copy(
+            cold.at[0, at], cold_v.at[0, pl.ds(lo, hi - lo)], first_sem.at[1, lo // early])
+
+    first_feat(0, early).start()
     state[3].start()
+    first_cold(0, early).start()
     state[4].start()
-    fetch(0)
+    if early < chunk:
+        first_feat(early, chunk).start()
+        first_cold(early, chunk).start()
     pl.semaphore_signal(barrier, inc=1, device_id={"dp": partner}, device_id_type=MESH)
 
     @pl.when(p > 0)
@@ -299,46 +317,59 @@
         def _():
             summed[at] = pack_a[2 * d + x, at]
 
-    def fill(i, first=0, last=chunk):
-        c = chunk_at(i)
-        grad = lax.dot_general(
+    def product(i, first=0, last=chunk):
+        return lax.dot_general(
             feat_v[i, :, first:last], og_v[...], (((0,), (0,)), ((), ())),
             preferred_element_type=jnp.float32,
         )
+
+    def sums(i, grad, first, g):
+        return [
+            grad[g - first:g - first + GROUP, b * LANES:(b + 1) * LANES]
+            + cold_v[i, g:g + GROUP, b * LANES:(b + 1) * LANES].astype(jnp.float32)
+            for b in range(blocks)
+        ]
+
+    def fill_hot(i, values, g):
+        c = chunk_at(i)
+        for r in range(hot):
+            cols = slice(r * LANES, (r + 1) * LANES)
+            held = values[0]
+            for b in range(1, blocks):
+                held = jnp.where(ranks[b] == r, values[b], held)
+            for h in range(0, GROUP, 8):
+                owner = c * inner + (g + h) // own
+                row = (g + h) % own
+                if row < cross_rows:
+                    pack_a[owner, row:row + 8, cols] = held[h:h + 8]
+                else:
+                    to = pl.ds(pl.multiple_of((owner % 2) * line_rows + row - cross_rows, 8), 8)
+                    pack_b[owner // 2, to, cols] = held[h:h + 8]
+
+    def fill_cold(i, values, g, squares):
+        at = pl.ds(pl.multiple_of(chunk_at(i) * chunk + g, 16), GROUP)
+        for b in range(blocks):
+            for h in range(0, GROUP, 8):
+                squares[b] += values[b][h:h + 8] * values[b][h:h + 8]
+            kept[at, b * LANES:(b + 1) * LANES] = jnp.where(
+                ranks[b] < hot, jnp.zeros_like(values[b]), values[b]).astype(jnp.bfloat16)
+
+    def fill(i, grad, first=0, last=chunk, hot_rows=True, cold_rows=True):
         squares = [sq[b] for b in range(blocks)]
         for g in range(first, last, GROUP):
-            values = []
+            values = sums(i, grad, first, g)
+            if cold_rows:
+                fill_cold(i, values, g, squares)
+            if hot_rows:
+                fill_hot(i, values, g)
+        if cold_rows:
             for b in range(blocks):
-                cols = slice(b * LANES, (b + 1) * LANES)
-                value = grad[g - first:g - first + GROUP, cols]
-                value += cold_v[i, g:g + GROUP, cols].astype(jnp.float32)
-                for h in range(0, GROUP, 8):
-                    squares[b] += value[h:h + 8] * value[h:h + 8]
-                values.append(value)
-            at = pl.ds(pl.multiple_of(c * chunk + g, 16), GROUP)
-            for b in range(blocks):
-                kept[at, b * LANES:(b + 1) * LANES] = jnp.where(
-                    ranks[b] < hot, jnp.zeros_like(values[b]), values[b]).astype(jnp.bfloat16)
-            for r in range(hot):
-                cols = slice(r * LANES, (r + 1) * LANES)
-                held = values[0]
-                for b in range(1, blocks):
-                    held = jnp.where(ranks[b] == r, values[b], held)
-                for h in range(0, GROUP, 8):
-                    owner = c * inner + (g + h) // own
-                    row = (g + h) % own
-                    if row < cross_rows:
-                        pack_a[owner, row:row + 8, cols] = held[h:h + 8]
-                    else:
-                        to = pl.ds(pl.multiple_of((owner % 2) * line_rows + row - cross_rows, 8), 8)
-                        pack_b[owner // 2, to, cols] = held[h:h + 8]
-        for b in range(blocks):
-            sq[b] = squares[b]
+                sq[b] = squares[b]
 
     def step(i):
         feat_copy(i).wait()
         cold_copy(i).wait()
-        fill(i)
+        fill(i, product(i))
         if chunk == own:
             send_cross(i)
             raw_b(dest(i // 2), chunk_at(i) % 2)
@@ -352,10 +383,10 @@
 
     state[4].wait()
     state[3].wait()
-    feat_copy(0).wait()
-    cold_copy(0).wait()
-    early = LANES if chunk == own else chunk
-    fill(0, 0, early)
+    first_feat(0, early).wait()
+    first_cold(0, early).wait()
+    grad = product(0, 0, early)
+    fill(0, grad, 0, early, cold_rows=False)
     greeted = (p + m - 1) // m + (2 * m - 2 - p) // m + 1 + (reps - 1)
     pl.semaphore_wait(barrier, greeted)
 
@@ -379,8 +410,12 @@
                     start_cross(0, sub)
 
         start_early(ready)
+    fill(0, grad, 0, early, hot_rows=False)
+    if chunk == own:
         if early < chunk:
-            fill(0, early, chunk)
+            first_feat(early, chunk).wait()
+            first_cold(early, chunk).wait()
+            fill(0, product(0, early, chunk), early, chunk)
         start_early(rest_of)
         raw_b(dest(0), 1 - x)
     rolled(1, chunks, step)

time: 48.6 us -> 48.4 us (level)
  no operation moved by 1% of the time
where the time goes in v7:
time: 48.4 us; the launch traced here: 48.1 us
  Pallas kernels  47.5 us (98%)
  between operations  0.64 us (1%)
    pallas_call x1, Pallas kernels, body(): pl.pallas_call(functools.partial(exchange_kernel, n, reps, hot), out_shap...  44.5 us
    pallas_call x1, Pallas kernels, body(): pl.pallas_call(functools.partial(update_kernel, n, rows * reps, tokens, h...  2.94 us

profile of v7, /device:TPU:0, one launch (start us, length us, event | category | flops | bytes accessed | tf_op | source)
XLA Modules:
  0.0 48.1 jit_solution(3051251901273661242)
XLA Ops:
  0.6 0.0 copy-start
  0.6 44.5 %exchange.1 = (f32[256,512]{1,0:T(8,128)S(1)}, f32[8,128]{1,0:T(8,128)S(1)}, bf16[2048,1024]{1,0:T(8,128)(2,1)S(1)}, f32[256,1024]{1,0:T(8,128)S(1)}, f32[256,1024]{1,0:T(8,128)S(1)}, /*index=5*/f32[256,1024]{1,0:T(8,128)S(1)}) custom-call(s32[8]{0:T(128)} %refs_0_.3, bf16[640,2048]{1,0:T(8,128)(2,1)} %refs_1_.1, bf16[640,1024]{1,0:T(8,128)(2,1)} %refs_2_.1, ...), custom_call_target="tpu_custom_call" | custom-call | tf_op jit(solution)/shard_map/exchange/pallas_call | solution.py:631
  45.2 0.0 copy-done
  45.2 2.9 %update.1 = (f32[256,1024]{1,0:T(8,128)}, f32[256,1024]{1,0:T(8,128)}, f32[256,1024]{1,0:T(8,128)}, bf16[1,2048,1024]{2,1,0:T(8,128)(2,1)}, f32[8,128]{1,0:T(8,128)}) custom-call(s32[8]{0:T(128)S(1)} %copy-done, f32[256,512]{1,0:T(8,128)S(1)} %get-tuple-element.16.refs_1_, f32[8,128]{1,0:T(8,128)S(1)} %get-tuple-element.17.refs_2_, ...), custom_call_target="tpu_custom_call" | custom-call | tf_op jit(solution)/shard_map/update/pallas_call | solution.py:666
Async XLA Ops:
  0.6 44.5 %copy-start = (s32[8]{0:T(128)S(1)}, s32[8]{0:T(128)}, u32[]{:S(2)}) copy-start(s32[8]{0:T(128)} %refs_0_.3) | copy-start | bytes 100

commit v8 on v7

--- a/solution.py
+++ b/solution.py
@@ -9,7 +9,7 @@
 LANES = 128
 GROUP = 32
 EXTRA = 86
-LAG = 1
+LAG = 0
 FRONT = 6
 VMEM_GRANT = 55 * 2**20
 MESH = pl.DeviceIdType.MESH
@@ -20,6 +20,8 @@
     cross = own - line
     extra = 8 * max(round(own / EXTRA), 1)
     head = 8 * ((cross - extra + 8) // 16)
+    if own > LANES:
+        head = min(head, LANES - line)
     return cross, line, ((0, head), (head, cross - extra - head), (cross - extra, extra))
 
 
@@ -91,6 +93,7 @@
     subs_all = range(len(pieces))
     kept_rows, extra_rows = pieces[-1]
     extra = slice(kept_rows, cross_rows)
+    head_rows = pieces[0][1]
     me = lax.axis_index("dp")
     rep = lax.axis_index("rep")
     x = me % 2
@@ -272,6 +275,7 @@
         def _():
             along_b(d, s, True).start()
 
+    def raw_e(d, s):
         @pl.when((d == m - 1) & (d > p) & (p == 0))
         def _():
             along_e(s).start()
@@ -315,7 +319,8 @@
 
         @pl.when(d == p)
         def _():
-            summed[at] = pack_a[2 * d + x, at]
+            moved = line_rows if sub else 0
+            summed[at.start + moved:at.stop + moved] = pack_a[2 * d + x, at]
 
     def product(i, first=0, last=chunk):
         return lax.dot_general(
@@ -340,11 +345,12 @@
             for h in range(0, GROUP, 8):
                 owner = c * inner + (g + h) // own
                 row = (g + h) % own
-                if row < cross_rows:
+                if head_rows <= row < head_rows + line_rows:
+                    to = pl.ds(pl.multiple_of((owner % 2) * line_rows + row - head_rows, 8), 8)
+                    pack_b[owner // 2, to, cols] = held[h:h + 8]
+                else:
+                    row = row if row < head_rows else row - line_rows
                     pack_a[owner, row:row + 8, cols] = held[h:h + 8]
-                else:
-                    to = pl.ds(pl.multiple_of((owner % 2) * line_rows + row - cross_rows, 8), 8)
-                    pack_b[owner // 2, to, cols] = held[h:h + 8]
 
     def fill_cold(i, values, g, squares):
         at = pl.ds(pl.multiple_of(chunk_at(i) * chunk + g, 16), GROUP)
@@ -373,6 +379,7 @@
         if chunk == own:
             send_cross(i)
             raw_b(dest(i // 2), chunk_at(i) % 2)
+            raw_e(dest(i // 2), chunk_at(i) % 2)
 
     def send_cross(i):
         k = (i - lag) // 2
@@ -410,6 +417,7 @@
                     start_cross(0, sub)
 
         start_early(ready)
+        raw_b(dest(0), 1 - x)
     fill(0, grad, 0, early, hot_rows=False)
     if chunk == own:
         if early < chunk:
@@ -417,7 +425,7 @@
             first_cold(early, chunk).wait()
             fill(0, product(0, early, chunk), early, chunk)
         start_early(rest_of)
-        raw_b(dest(0), 1 - x)
+        raw_e(dest(0), 1 - x)
     rolled(1, chunks, step)
     for copy in state[:3]:
         copy.start()
@@ -429,6 +437,7 @@
                     start_cross(k, sub)
             for s in range(2):
                 raw_b(dest(k), s)
+                raw_e(dest(k), s)
 
         rolled(0, m, launch)
     for r in range(blocks):
@@ -528,12 +537,12 @@
     cross_step(m - 1)
     cross_b().wait_recv()
     mine = pl.ds(pl.multiple_of(x * line_rows, 8), line_rows)
-    summed[cross_rows:] = pack_b[p, mine] + rx_b[...]
+    summed[head_rows:head_rows + line_rows] = pack_b[p, mine] + rx_b[...]
 
     @pl.when(p == m - 1)
     def _():
         cross_e().wait_recv()
-        summed[extra] = pack_a[2 * p + x, extra] + rx_e[...]
+        summed[own - extra_rows:] = pack_a[2 * p + x, extra] + rx_e[...]
         cross_e().wait_send()
 
 

time: 48.4 us -> 48.1 us (level)
  no operation moved by 1% of the time
where the time goes in v8:
time: 48.1 us; the launch traced here: 47.9 us
  Pallas kernels  47.3 us (98%)
  between operations  0.66 us (1%)
    pallas_call x1, Pallas kernels, body(): pl.pallas_call(functools.partial(exchange_kernel, n, reps, hot), out_shap...  44.3 us
    pallas_call x1, Pallas kernels, body(): pl.pallas_call(functools.partial(update_kernel, n, rows * reps, tokens, h...  2.94 us

profile of v8, /device:TPU:0, one launch (start us, length us, event | category | flops | bytes accessed | tf_op | source)
XLA Modules:
  0.0 47.9 jit_solution(14688406264486492439)
XLA Ops:
  0.6 0.0 copy-start
  0.6 44.3 %exchange.1 = (f32[256,512]{1,0:T(8,128)S(1)}, f32[8,128]{1,0:T(8,128)S(1)}, bf16[2048,1024]{1,0:T(8,128)(2,1)S(1)}, f32[256,1024]{1,0:T(8,128)S(1)}, f32[256,1024]{1,0:T(8,128)S(1)}, /*index=5*/f32[256,1024]{1,0:T(8,128)S(1)}) custom-call(s32[8]{0:T(128)} %refs_0_.3, bf16[640,2048]{1,0:T(8,128)(2,1)} %refs_1_.1, bf16[640,1024]{1,0:T(8,128)(2,1)} %refs_2_.1, ...), custom_call_target="tpu_custom_call" | custom-call | tf_op jit(solution)/shard_map/exchange/pallas_call | solution.py:640
  45.0 0.0 copy-done
  45.0 2.9 %update.1 = (f32[256,1024]{1,0:T(8,128)}, f32[256,1024]{1,0:T(8,128)}, f32[256,1024]{1,0:T(8,128)}, bf16[1,2048,1024]{2,1,0:T(8,128)(2,1)}, f32[8,128]{1,0:T(8,128)}) custom-call(s32[8]{0:T(128)S(1)} %copy-done, f32[256,512]{1,0:T(8,128)S(1)} %get-tuple-element.16.refs_1_, f32[8,128]{1,0:T(8,128)S(1)} %get-tuple-element.17.refs_2_, ...), custom_call_target="tpu_custom_call" | custom-call | tf_op jit(solution)/shard_map/update/pallas_call | solution.py:675
Async XLA Ops:
  0.6 44.3 %copy-start = (s32[8]{0:T(128)S(1)}, s32[8]{0:T(128)}, u32[]{:S(2)}) copy-start(s32[8]{0:T(128)} %refs_0_.3) | copy-start | bytes 100

commit v9 on v8

--- a/solution.py
+++ b/solution.py
@@ -8,7 +8,7 @@
 
 LANES = 128
 GROUP = 32
-EXTRA = 86
+EXTRA = 64
 LAG = 0
 FRONT = 6
 VMEM_GRANT = 55 * 2**20

time: 48.1 us -> 48 us (level)
  no operation moved by 1% of the time
where the time goes in v9:
time: 48 us; the launch traced here: 47.9 us
  Pallas kernels  47.2 us (98%)
  between operations  0.64 us (1%)
    pallas_call x1, Pallas kernels, body(): pl.pallas_call(functools.partial(exchange_kernel, n, reps, hot), out_shap...  44.3 us
    pallas_call x1, Pallas kernels, body(): pl.pallas_call(functools.partial(update_kernel, n, rows * reps, tokens, h...  2.94 us

profile of v9, /device:TPU:0, one launch (start us, length us, event | category | flops | bytes accessed | tf_op | source)
XLA Modules:
  0.0 47.9 jit_solution(2560590378817327744)
XLA Ops:
  0.6 0.0 copy-start
  0.6 44.3 %exchange.1 = (f32[256,512]{1,0:T(8,128)S(1)}, f32[8,128]{1,0:T(8,128)S(1)}, bf16[2048,1024]{1,0:T(8,128)(2,1)S(1)}, f32[256,1024]{1,0:T(8,128)S(1)}, f32[256,1024]{1,0:T(8,128)S(1)}, /*index=5*/f32[256,1024]{1,0:T(8,128)S(1)}) custom-call(s32[8]{0:T(128)} %refs_0_.3, bf16[640,2048]{1,0:T(8,128)(2,1)} %refs_1_.1, bf16[640,1024]{1,0:T(8,128)(2,1)} %refs_2_.1, ...), custom_call_target="tpu_custom_call" | custom-call | tf_op jit(solution)/shard_map/exchange/pallas_call | solution.py:640
  44.9 0.0 copy-done
  44.9 2.9 %update.1 = (f32[256,1024]{1,0:T(8,128)}, f32[256,1024]{1,0:T(8,128)}, f32[256,1024]{1,0:T(8,128)}, bf16[1,2048,1024]{2,1,0:T(8,128)(2,1)}, f32[8,128]{1,0:T(8,128)}) custom-call(s32[8]{0:T(128)S(1)} %copy-done, f32[256,512]{1,0:T(8,128)S(1)} %get-tuple-element.16.refs_1_, f32[8,128]{1,0:T(8,128)S(1)} %get-tuple-element.17.refs_2_, ...), custom_call_target="tpu_custom_call" | custom-call | tf_op jit(solution)/shard_map/update/pallas_call | solution.py:675
Async XLA Ops:
  0.6 44.3 %copy-start = (s32[8]{0:T(128)S(1)}, s32[8]{0:T(128)}, u32[]{:S(2)}) copy-start(s32[8]{0:T(128)} %refs_0_.3) | copy-start | bytes 100
